TPU v7x, 32 devices: a whole 2x2x4 slice. The times are simulated.
32 devices in a mesh: rows: 4 (over x, core), cols: 8 (over z, y).
Axes of the slice: x: 2, y: 2, z: 4, core: 2. Of those that a mesh axis runs over, the one named last changes fastest.
Arguments:
- design: bfloat16 [4096, 8192], P('rows', 'cols'), may hold values from -6 to 6
- theta: float32 [8192], P('cols'), may hold values from -0.0625 to 0.0625
- feature_scale: float32 [8192], P('cols'), may hold values from 0.05 to 2
- labels: int32 [4096], P('rows'), may hold values 0 or 1
- psi: bfloat16 [1024, 256], replicated, may hold values from -0.1875 to 0.1875
- phi: float32 [512, 256], replicated, may hold values from -0.25 to 0.25
Outputs:
- newton_step: float32 [8192], P('cols')
- sketch: float32 [256, 8192], P(None, 'cols')
All inputs are finite; a program needn't handle non-finite values. No bound on the sum of `labels` on one device may be relied on, other than what follows from the above.
Results may differ from a plain program's by a relative error of at most 0.0085.
Values sent between devices are 32-bit elements; how exact they have to be, the bound alone decides.
No kernel may reach another device: no remote copies, remote signals or barrier semaphores. Data moves between devices by JAX's collectives and lax.ppermute only.
A program may use at most 128 MiB of HBM per device.

v0:
```python
import jax
import jax.numpy as jnp
from jax import lax
from jax.sharding import PartitionSpec as P

ITERS = 10


damping = 0.01
shrink_share = 0.05
highest = lax.Precision.HIGHEST


def swapped(value, axis, stride):
    mask = 2**stride
    pairs = [(source, source ^ mask) for source in range(lax.axis_size(axis))]
    return lax.ppermute(value, axis, pairs)


def shrink_weights(range_rows):
    width = range_rows.shape[1]
    moment = jnp.dot(range_rows.T, range_rows, precision=highest)
    ridge = shrink_share * jnp.trace(moment) / width
    factor = jnp.linalg.cholesky(moment + ridge * jnp.eye(width, dtype=jnp.float32))
    return jax.scipy.linalg.solve_triangular(factor, range_rows.T, lower=True)


def on_device(design, theta, feature_scale, labels, psi, phi):
    row_devices = lax.axis_size("rows")
    samples = design.shape[0] * row_devices
    width = psi.shape[1]
    scaled_theta = (theta * feature_scale).astype(jnp.bfloat16)
    margins = lax.psum(jnp.dot(design, scaled_theta, preferred_element_type=jnp.float32), "cols")
    chance = jax.nn.sigmoid(margins)
    weight = chance * (1.0 - chance)
    misfit = (chance - labels.astype(jnp.float32)).astype(jnp.bfloat16)
    summed_grad = lax.psum(jnp.dot(misfit, design, preferred_element_type=jnp.float32), "rows")
    gradient = feature_scale * summed_grad / samples + damping * theta
    rows_scaled = (
        design.astype(jnp.float32) * jnp.sqrt(weight)[:, None] * feature_scale[None, :]
    ).astype(jnp.bfloat16)
    mixed_cols = jnp.einsum(
        "rf,rs->fs", rows_scaled, psi, preferred_element_type=jnp.float32
    ).astype(jnp.bfloat16)
    range_rows = lax.psum(
        jnp.dot(rows_scaled, mixed_cols, preferred_element_type=jnp.float32), "cols"
    )
    leaf_weights = shrink_weights(range_rows).astype(jnp.bfloat16)
    sketch = jnp.dot(leaf_weights, rows_scaled, preferred_element_type=jnp.float32)
    position = lax.axis_index("rows")
    for level_bit in range(row_devices.bit_length() - 1):
        partner = swapped(sketch, "rows", level_bit)
        first_low = position // (1 << level_bit) % 2 == 0
        lower_half = jnp.where(first_low, sketch, partner)
        upper_half = jnp.where(first_low, partner, sketch)
        stacked = jnp.concatenate([lower_half, upper_half], 0)
        gram = lax.psum(jnp.dot(stacked, stacked.T, precision=highest), "cols")
        range_rows = jnp.dot(gram, phi, precision=highest)
        sketch = jnp.dot(shrink_weights(range_rows), stacked, precision=highest)
    kernel_part = lax.psum(jnp.dot(sketch, sketch.T, precision=highest), "cols")
    kernel = kernel_part + damping * samples * jnp.eye(width, dtype=jnp.float32)
    kernel_factor = jnp.linalg.cholesky(kernel)
    solution = jnp.zeros_like(gradient)
    residual = gradient

    def precondition_plus(vector):
        projected, squared = lax.psum(
            (jnp.dot(sketch, vector, precision=highest), jnp.sum(vector * vector)), "cols"
        )
        solved = jax.scipy.linalg.cho_solve((kernel_factor, True), projected)
        smoothed = (vector - jnp.dot(solved, sketch, precision=highest)) / damping
        return (smoothed, (squared - jnp.sum(projected * solved)) / damping)

    search, agreement = precondition_plus(residual)
    for turn_index in range(ITERS):
        rounded = (feature_scale * search).astype(jnp.bfloat16)
        forward_rows, length = lax.psum(
            (
                jnp.dot(design, rounded, preferred_element_type=jnp.float32),
                jnp.sum(search * search),
            ),
            "cols",
        )
        inner = (weight * forward_rows).astype(jnp.bfloat16)
        back_sum, bending = lax.psum(
            (
                jnp.dot(inner, design, preferred_element_type=jnp.float32),
                jnp.sum(forward_rows * inner.astype(jnp.float32)),
            ),
            "rows",
        )
        product = feature_scale * back_sum / samples + damping * search
        product, curvature = (product, bending / samples + damping * length)
        step_size = agreement / curvature
        solution = solution + step_size * search
        residual = residual - step_size * product
        if turn_index + 1 < ITERS:
            smoothed, agreement_next = precondition_plus(residual)
            search = smoothed + agreement_next / agreement * search
            agreement = agreement_next
    return (solution, sketch)


def solution(mesh):
    in_specs = (P("rows", "cols"), P("cols"), P("cols"), P("rows"), P(), P())
    out_specs = (P("cols"), P(None, "cols"))
    return jax.shard_map(
        on_device, mesh=mesh, in_specs=in_specs, out_specs=out_specs, check_vma=False
    )
```

profile of v0, /device:TPU:0, one launch (start us, length us, event | category | flops | bytes accessed | tf_op | source)
XLA Modules:
  0.0 1238.0 jit_solution(12997754419069925355)
XLA Ops:
  10.4 23.2 %psum.455 = f32[1024]{0:T(1024)S(1)} all-reduce(f32[1024]{0:T(1024)S(1)} %bitcast.779), channel_id=1, replica_groups=mesh['rows'=4,'cols'=8] {'cols'}, use_global_device_ids=true, to_apply=%region_0.0 | all-reduce | flops 1024 | bytes 8192 | tf_op jit(solution)/shard_map/psum | solution.py:33
  37.7 75.0 %all-reduce.34.cloned.1.call-done = f32[1024,256]{1,0:T(8,128)} async-done(((f32[1024,256]{1,0:T(8,128)}), f32[1024,256]{1,0:T(8,128)}) %all-reduce.34.cloned.1.call-update) | async-done | bytes 1048592 | tf_op jit(solution)/shard_map/psum | solution.py:45
  158.9 19.7 %custom-call.20 = f32[2,128,128]{1,2,0:T(8,128)S(1)} custom-call(f32[2,128,128]{2,1,0:T(8,128)S(1)} %get-tuple-element.28), custom_call_target="InvertDiagBlocksLowerTriangular" | custom-call | tf_op jit(solution)/shard_map/jit(_solve_triangular)/triangular_solve | solution.py:25
  195.9 77.6 %all-reduce.36.cloned.1.call-done = f32[512,512]{1,0:T(8,128)} async-done(((f32[512,512]{1,0:T(8,128)}), f32[512,512]{1,0:T(8,128)}) %all-reduce.36.cloned.1.call-update) | async-done | bytes 1048592 | tf_op jit(solution)/shard_map/psum | solution.py:57
  328.4 20.5 %custom-call.36 = f32[2,128,128]{1,2,0:T(8,128)S(1)} custom-call(f32[2,128,128]{2,1,0:T(8,128)} %copy-done.15), custom_call_target="InvertDiagBlocksLowerTriangular" | custom-call | tf_op jit(solution)/shard_map/jit(_solve_triangular)/triangular_solve | solution.py:25
  355.9 23.7 %collective-permute-done.1 = f32[256,1024]{1,0:T(8,128)} collective-permute-done((f32[256,1024]{1,0:T(8,128)}, f32[256,1024]{1,0:T(8,128)}, u32[]{:S(2)}, u32[]{:S(2)}) %collective-permute-start.1) | collective-permute-done | bytes 1048608 | tf_op jit(solution)/shard_map/ppermute | solution.py:17
  393.5 71.1 %all-reduce.38.cloned.1.call-done = f32[512,512]{1,0:T(8,128)} async-done(((f32[512,512]{1,0:T(8,128)}), f32[512,512]{1,0:T(8,128)}) %all-reduce.38.cloned.1.call-update) | async-done | bytes 1048592 | tf_op jit(solution)/shard_map/psum | solution.py:57
  519.8 20.5 %custom-call.38 = f32[2,128,128]{1,2,0:T(8,128)S(1)} custom-call(f32[2,128,128]{2,1,0:T(8,128)} %copy-done.16), custom_call_target="InvertDiagBlocksLowerTriangular" | custom-call | tf_op jit(solution)/shard_map/jit(_solve_triangular)/triangular_solve | solution.py:25
  550.4 20.2 %psum.461 = f32[256]{0:T(256)S(1)} all-reduce(f32[256]{0:T(256)S(1)} %bitcast.781), channel_id=1, replica_groups=mesh['rows'=4,'cols'=8] {'cols'}, use_global_device_ids=true, to_apply=%region_13.16 | all-reduce | flops 256 | bytes 2048 | tf_op jit(solution)/shard_map/psum | solution.py:67
  570.7 47.8 %all-reduce.40.cloned.1.call-done = f32[256,256]{0,1:T(8,128)} async-done(((f32[256,256]{0,1:T(8,128)}), f32[256,256]{0,1:T(8,128)}) %all-reduce.40.cloned.1.call-update) | async-done | bytes 262160 | tf_op jit(solution)/shard_map/psum | solution.py:60
  662.5 19.9 %custom-call.40 = f32[2,128,128]{1,2,0:T(8,128)S(1)} custom-call(f32[2,128,128]{2,1,0:T(8,128)S(1)} %get-tuple-element.91), custom_call_target="InvertDiagBlocksLowerTriangular" | custom-call | tf_op jit(solution)/shard_map/jit(_cho_solve)/triangular_solve | solution.py:70
  686.6 20.6 %all-reduce.19 = (f32[1024]{0:T(1024)S(1)}, f32[]{:T(128)}, f32[]{:T(128)}) all-reduce(f32[1024]{0:T(1024)S(1)} %bitcast.760, f32[]{:T(128)} %get-tuple-element.250, f32[]{:T(128)} %get-tuple-element.248), channel_id=1, replica_groups=mesh['rows'=4,'cols'=8] {'cols'}, use_global_device_ids=true, to_apply=%region_17.21 | all-reduce | flops 1026 | bytes 8208 | tf_op jit(solution)/shard_map/psum | solution.py:77
  744.7 20.0 %all-reduce.17 = (f32[1024]{0:T(1024)S(1)}, f32[]{:T(128)}) all-reduce(f32[1024]{0:T(1024)S(1)} %bitcast.762, f32[]{:T(128)} %get-tuple-element.242), channel_id=1, replica_groups=mesh['rows'=4,'cols'=8] {'cols'}, use_global_device_ids=true, to_apply=%region_27.31 | all-reduce | flops 1025 | bytes 8200 | tf_op jit(solution)/shard_map/psum | solution.py:77
  776.3 17.8 %all-reduce.16 = (f32[256]{0:T(256)S(1)}, f32[]{:T(128)}) all-reduce(f32[256]{0:T(256)S(1)} %bitcast.793, f32[]{:T(128)} %get-tuple-element.238), channel_id=1, replica_groups=mesh['rows'=4,'cols'=8] {'cols'}, use_global_device_ids=true, to_apply=%region_35.39 | all-reduce | flops 257 | bytes 2056 | tf_op jit(solution)/shard_map/psum | solution.py:67
  800.3 20.0 %all-reduce.15 = (f32[1024]{0:T(1024)S(1)}, f32[]{:T(128)}) all-reduce(f32[1024]{0:T(1024)S(1)} %bitcast.764, f32[]{:T(128)} %get-tuple-element.236), channel_id=1, replica_groups=mesh['rows'=4,'cols'=8] {'cols'}, use_global_device_ids=true, to_apply=%region_37.41 | all-reduce | flops 1025 | bytes 8200 | tf_op jit(solution)/shard_map/psum | solution.py:77
  831.9 18.2 %all-reduce.14 = (f32[256]{0:T(256)S(1)}, f32[]{:T(128)}) all-reduce(f32[256]{0:T(256)S(1)} %bitcast.794, f32[]{:T(128)} %get-tuple-element.232), channel_id=1, replica_groups=mesh['rows'=4,'cols'=8] {'cols'}, use_global_device_ids=true, to_apply=%region_45.49 | all-reduce | flops 257 | bytes 2056 | tf_op jit(solution)/shard_map/psum | solution.py:67
  858.0 20.0 %all-reduce.13 = (f32[1024]{0:T(1024)S(1)}, f32[]{:T(128)}) all-reduce(f32[1024]{0:T(1024)S(1)} %bitcast.766, f32[]{:T(128)} %get-tuple-element.230), channel_id=1, replica_groups=mesh['rows'=4,'cols'=8] {'cols'}, use_global_device_ids=true, to_apply=%region_47.51 | all-reduce | flops 1025 | bytes 8200 | tf_op jit(solution)/shard_map/psum | solution.py:77
  915.2 20.0 %all-reduce.11 = (f32[1024]{0:T(1024)S(1)}, f32[]{:T(128)}) all-reduce(f32[1024]{0:T(1024)S(1)} %bitcast.768, f32[]{:T(128)} %get-tuple-element.224), channel_id=1, replica_groups=mesh['rows'=4,'cols'=8] {'cols'}, use_global_device_ids=true, to_apply=%region_57.61 | all-reduce | flops 1025 | bytes 8200 | tf_op jit(solution)/shard_map/psum | solution.py:77
  972.5 20.0 %all-reduce.9 = (f32[1024]{0:T(1024)S(1)}, f32[]{:T(128)}) all-reduce(f32[1024]{0:T(1024)S(1)} %bitcast.770, f32[]{:T(128)} %get-tuple-element.218), channel_id=1, replica_groups=mesh['rows'=4,'cols'=8] {'cols'}, use_global_device_ids=true, to_apply=%region_67.71 | all-reduce | flops 1025 | bytes 8200 | tf_op jit(solution)/shard_map/psum | solution.py:77
  1029.8 20.0 %all-reduce.7 = (f32[1024]{0:T(1024)S(1)}, f32[]{:T(128)}) all-reduce(f32[1024]{0:T(1024)S(1)} %bitcast.772, f32[]{:T(128)} %get-tuple-element.212), channel_id=1, replica_groups=mesh['rows'=4,'cols'=8] {'cols'}, use_global_device_ids=true, to_apply=%region_77.81 | all-reduce | flops 1025 | bytes 8200 | tf_op jit(solution)/shard_map/psum | solution.py:77
  1061.4 17.9 %all-reduce.6 = (f32[256]{0:T(256)S(1)}, f32[]{:T(128)}) all-reduce(f32[256]{0:T(256)S(1)} %bitcast.798, f32[]{:T(128)} %get-tuple-element.208), channel_id=1, replica_groups=mesh['rows'=4,'cols'=8] {'cols'}, use_global_device_ids=true, to_apply=%region_85.89 | all-reduce | flops 257 | bytes 2056 | tf_op jit(solution)/shard_map/psum | solution.py:67
  1087.3 20.0 %all-reduce.5 = (f32[1024]{0:T(1024)S(1)}, f32[]{:T(128)}) all-reduce(f32[1024]{0:T(1024)S(1)} %bitcast.774, f32[]{:T(128)} %get-tuple-element.206), channel_id=1, replica_groups=mesh['rows'=4,'cols'=8] {'cols'}, use_global_device_ids=true, to_apply=%region_87.91 | all-reduce | flops 1025 | bytes 8200 | tf_op jit(solution)/shard_map/psum | solution.py:77
  1144.6 20.0 %all-reduce.3 = (f32[1024]{0:T(1024)S(1)}, f32[]{:T(128)}) all-reduce(f32[1024]{0:T(1024)S(1)} %bitcast.776, f32[]{:T(128)} %get-tuple-element.200), channel_id=1, replica_groups=mesh['rows'=4,'cols'=8] {'cols'}, use_global_device_ids=true, to_apply=%region_97.101 | all-reduce | flops 1025 | bytes 8200 | tf_op jit(solution)/shard_map/psum | solution.py:77
  1202.1 20.0 %all-reduce.1 = (f32[1024]{0:T(1024)S(1)}, f32[]{:T(128)}) all-reduce(f32[1024]{0:T(1024)S(1)} %bitcast.778, f32[]{:T(128)} %get-tuple-element.194), channel_id=1, replica_groups=mesh['rows'=4,'cols'=8] {'cols'}, use_global_device_ids=true, to_apply=%region_107.111 | all-reduce | flops 1025 | bytes 8200 | tf_op jit(solution)/shard_map/psum | solution.py:77
  (378 shorter events, 536.5 us)
Async XLA Ops:
  7.2 26.4 %copy-start = (bf16[1024,256]{1,0:T(8,128)(2,1)S(1)}, bf16[1024,256]{1,0:T(8,128)(2,1)}, u32[]{:S(2)}) copy-start(bf16[1024,256]{1,0:T(8,128)(2,1)} %param.15) | copy-start | bytes 1572868
  7.2 26.4 %copy-start.10 = (f32[1024]{0:T(1024)S(1)}, f32[1024]{0:T(1024)}, u32[]{:S(2)}) copy-start(f32[1024]{0:T(1024)} %param.13) | copy-start | bytes 12292
  7.2 26.4 %copy-start.1 = (bf16[1024,1024]{1,0:T(8,128)(2,1)S(1)}, bf16[1024,1024]{1,0:T(8,128)(2,1)}, u32[]{:S(2)}) copy-start(bf16[1024,1024]{1,0:T(8,128)(2,1)} %param.11) | copy-start | bytes 6291460
  7.2 26.3 %copy-start.18 = (s32[1024]{0:T(1024)S(1)}, s32[1024]{0:T(1024)}, u32[]{:S(2)}) copy-start(s32[1024]{0:T(1024)} %param.14) | copy-start | bytes 12292
  7.2 105.5 %all-reduce.34.cloned.1.call-start = ((), (), s32[]{:S(2)}) async-start(), calls=%async_computation | async-start | bytes 2097152 | tf_op jit(solution)/shard_map/psum | solution.py:45
  36.9 236.5 %all-reduce.36.cloned.1.call-start = ((), (), s32[]{:S(2)}) async-start(), calls=%async_computation.1 | async-start | bytes 2097152 | tf_op jit(solution)/shard_map/psum | solution.py:57
  158.9 19.7 %copy-start.19 = (s32[2,2]{1,0:T(2,128)}, s32[2,2]{1,0:T(2,128)S(1)}, u32[]{:S(2)}) copy-start(s32[2,2]{1,0:T(2,128)S(1)} %get-tuple-element.492) | copy-start | bytes 52
  184.9 3.0 collective-permute-start
  189.6 1.0 copy-start.7
  189.6 1.3 copy-start.9
  195.4 269.2 %all-reduce.38.cloned.1.call-start = ((), (), s32[]{:S(2)}) async-start(), calls=%async_computation.2 | async-start | bytes 2097152 | tf_op jit(solution)/shard_map/psum | solution.py:57
  281.7 0.7 copy-start.13
  318.7 2.6 copy-start.11
  348.9 1.5 copy-start.8
  354.5 25.2 %collective-permute-start.1 = (f32[256,1024]{1,0:T(8,128)}, f32[256,1024]{1,0:T(8,128)}, u32[]{:S(2)}, u32[]{:S(2)}) collective-permute-start(f32[256,1024]{1,0:T(8,128)} %fusion.2), channel_id=1, source_target_pairs={{0,16},{8,24},{16,0},{24,8},{1,17},{9,25},{17,1},{25,9},{2,18},{10... | collective-permute-start | bytes 3145736 | tf_op jit(solution)/shard_map/ppermute | solution.py:17
  381.3 1.0 copy-start.4
  381.3 1.3 copy-start.6
  387.2 231.2 %all-reduce.40.cloned.1.call-start = ((), (), s32[]{:S(2)}) async-start(), calls=%async_computation.3 | async-start | bytes 524288 | tf_op jit(solution)/shard_map/psum | solution.py:60
  472.9 0.7 copy-start.14
  510.1 2.6 copy-start.12
  540.3 1.5 copy-start.5
  544.9 1.0 copy-start.2
  545.8 1.8 copy-start.17
  662.5 132.4 %copy-start.3 = (f32[256,256]{1,0:T(8,128)}, f32[256,256]{1,0:T(8,128)S(1)}, u32[]{:S(2)}) copy-start(f32[256,256]{1,0:T(8,128)S(1)} %get-tuple-element.476) | copy-start | bytes 786436
  (2 other events, 1.3 us)
Sparse Core Ops, SparseCore 0:
  37.0 75.6 all-reduce.33
  195.6 77.8 all-reduce.35
  387.3 77.2 all-reduce.37
  547.7 70.6 all-reduce.39
where the time goes:
time: 1240 us
  blocking collectives  475 us (38%)
  waiting for transfers between devices  298 us (24%)
  other arithmetic  259 us (21%)
  matrix products  123 us (10%)
  between operations  48.3 us (4%)
  local copies, waits for them, and re-layouts  32.1 us (3%)
    psum x10, blocking collectives, on_device(): lax.psum((jnp.dot(design, rounded, preferred_element_type=jnp.float32), j...  201 us
    psum x10, blocking collectives, precondition_plus(): lax.psum((jnp.dot(sketch, vector, precision=highest), jnp.sum(vector * ve...  181 us
    psum x2, waiting for transfers between devices, on_device(): gram = lax.psum(jnp.dot(stacked, stacked.T, precision=highest), 'cols')  149 us
    another operation x20, other arithmetic, shrink_weights(): jnp.linalg.cholesky(moment + ridge * jnp.eye(width, dtype=jnp.float32))  105 us
    psum x1, waiting for transfers between devices, on_device(): lax.psum(jnp.dot(rows_scaled, mixed_cols, preferred_element_type=jnp.floa...  75 us
    psum x10, blocking collectives, on_device(): lax.psum((jnp.dot(inner, design, preferred_element_type=jnp.float32), jnp...  64.5 us
    another operation x7, other arithmetic, shrink_weights(): return jax.scipy.linalg.solve_triangular(factor, range_rows.T, lower=True)  63.2 us
    psum x1, waiting for transfers between devices, on_device(): kernel_part = lax.psum(jnp.dot(sketch, sketch.T, precision=highest), 'cols')  47.8 us
  transfers between devices with their start and end apart: 6, of which 6 were waited for; matrix products, arithmetic and copies ran while one was open for 0% of the time, Pallas kernels for 0%

commit v1 on v0

v1 whole, which is shorter than its diff:
```python
import functools

import jax
import jax.numpy as jnp
from jax import lax
from jax.experimental import pallas as pl
from jax.experimental.pallas import tpu as pltpu
from jax.sharding import PartitionSpec as P

ITERS = 10


damping = 0.01
shrink_share = 0.05
highest = lax.Precision.HIGHEST
LANES = 128
BLOCK = 16
NT = (((1,), (1,)), ((), ()))
NN = (((1,), (0,)), ((), ()))
TN = (((0,), (0,)), ((), ()))


def swapped(value, axis, stride):
    mask = 2**stride
    pairs = [(source, source ^ mask) for source in range(lax.axis_size(axis))]
    return lax.ppermute(value, axis, pairs)


def shrink_weights(range_rows):
    moment = jnp.dot(range_rows.T, range_rows, precision=highest)
    return jnp.dot(inverse_factor(moment, shrink_share), range_rows.T, precision=highest)


def split(value, parts):
    out = []
    for _ in range(parts):
        piece = value.astype(jnp.bfloat16)
        out.append(piece)
        value = value - piece.astype(jnp.float32)
    return out


def factor_kernel(share, m_ref, w_ref, a_ref):
    n = m_ref.shape[0]
    row = lax.broadcasted_iota(jnp.int32, (n, n), 0)
    lane = lax.broadcasted_iota(jnp.int32, (n, n), 1)
    m = m_ref[...]
    diag = jnp.where(row == lane, m, 0.0)
    trace = jnp.sum(jnp.sum(diag, axis=0, keepdims=True), axis=1, keepdims=True)
    a_ref[...] = m + jnp.where(row == lane, share * trace / n, 0.0)
    sub = lax.broadcasted_iota(jnp.int32, (BLOCK, LANES), 0)
    wide_sub = lax.broadcasted_iota(jnp.int32, (BLOCK, n), 0)
    wide_lane = lax.broadcasted_iota(jnp.int32, (BLOCK, n), 1)
    for half in range(n // LANES):
        first_row = half * LANES

        def step(block, carry):
            base = half * LANES + block * BLOCK
            panel = a_ref[pl.ds(pl.multiple_of(base, BLOCK), BLOCK), :]
            tile = panel[:, half * LANES : (half + 1) * LANES]
            tile = pltpu.roll(tile, (LANES - block * BLOCK) % LANES, 1)
            cols = [jnp.broadcast_to(tile[:, m : m + 1], (BLOCK, LANES)) for m in range(BLOCK)]
            inside = (wide_lane >= base) & (wide_lane < base + BLOCK)
            panel = jnp.where(inside, jnp.where(wide_lane - base == wide_sub, 1.0, 0.0), panel)
            scale = jnp.zeros((BLOCK, LANES), jnp.float32)
            for k in range(BLOCK):
                pivot = jnp.broadcast_to(cols[k][k : k + 1], (BLOCK, LANES))
                inverse = 1.0 / pivot
                scale = jnp.where(sub == k, lax.rsqrt(pivot), scale)
                factor = jnp.where(sub > k, cols[k], 0.0) * inverse
                panel = panel - jnp.concatenate([factor] * (n // LANES), 1) * panel[k : k + 1]
                for m in range(k + 1, BLOCK):
                    cols[m] = cols[m] - factor * cols[k][m : m + 1]
            panel = panel * jnp.concatenate([scale] * (n // LANES), 1)
            a_ref[pl.ds(pl.multiple_of(base, BLOCK), BLOCK), :] = panel
            after = jnp.where(wide_lane >= base + BLOCK, panel, 0.0)[:, first_row:]
            l0, l1, l2 = split(after, 3)
            r0, r1, r2 = split(panel, 3)
            left = jnp.concatenate([l0, l0, l1, l0, l1, l2], 0)
            right = jnp.concatenate([r0, r1, r0, r2, r1, r0], 0)
            update = lax.dot_general(left, right, TN, preferred_element_type=jnp.float32)
            old = a_ref[first_row:, :]
            lane_here, row_here = lane[first_row:], row[first_row:]
            gone = (lane_here >= base) & (lane_here < base + BLOCK) & (row_here >= base + BLOCK)
            a_ref[first_row:, :] = jnp.where(gone, 0.0, old) - update
            return carry

        lax.fori_loop(0, LANES // BLOCK, step, 0)
    w_ref[...] = jnp.where(lane <= row, a_ref[...], 0.0)

def inverse_factor(m, share):
    n = m.shape[0]
    return pl.pallas_call(
        functools.partial(factor_kernel, share),
        out_shape=jax.ShapeDtypeStruct((n, n), jnp.float32),
        in_specs=[pl.BlockSpec(memory_space=pltpu.VMEM)],
        out_specs=pl.BlockSpec(memory_space=pltpu.VMEM),
        scratch_shapes=[pltpu.VMEM((n, n), jnp.float32)],
        cost_estimate=pl.CostEstimate(flops=20_000_000, bytes_accessed=600_000, transcendentals=0),
    )(m)


def stacked_splits(row):
    n = row.shape[1]
    high = row.astype(jnp.bfloat16).astype(jnp.float32)
    rest = row - high
    mid = rest.astype(jnp.bfloat16).astype(jnp.float32)
    low = rest - mid
    at = lax.broadcasted_iota(jnp.int32, (8, n), 0)
    full = jnp.where(at == 0, high, jnp.where(at == 1, mid, jnp.where(at == 2, low, 0.0)))
    return full.astype(jnp.bfloat16)


def row_dot(stack, matrices, dims):
    total = None
    for matrix in matrices:
        part = lax.dot_general(stack, matrix, dims, preferred_element_type=jnp.float32)
        total = part if total is None else total + part
    return jnp.sum(total, axis=0, keepdims=True)


def put_scalars(values):
    at = lax.broadcasted_iota(jnp.int32, (1, LANES), 1)
    row = jnp.zeros((1, LANES), jnp.float32)
    for index, value in enumerate(values):
        row = jnp.where(at == index, value, row)
    return row


def total(row):
    return jnp.sum(row, axis=1, keepdims=True)


def forward_kernel(samples, first, *refs):
    if first:
        (grad_ref, q_ref, scale_ref, design_ref, s0_ref, s1_ref, inv_ref, vec_out, small_out, msg_out) = refs
        r = grad_ref[...]
        x = jnp.zeros_like(r)
        q = q_ref[...]
    else:
        (at_ref, msg_ref, vec_ref, small_ref, scales_ref, scale_ref, design_ref, s0_ref, s1_ref, inv_ref, vec_out, small_out, msg_out) = refs
        groups, n_col = msg_ref.shape[0], msg_ref.shape[1]
        feats = scale_ref.shape[1]
        width = inv_ref.shape[1]
        here = at_ref[0]
        squares = jnp.zeros((1, feats), jnp.float32)
        tail = jnp.zeros((1, width + LANES), jnp.float32)
        for col in range(n_col):
            back = msg_ref[0, col, :, :feats]
            tail = tail + msg_ref[0, col, :, feats:]
            for group in range(1, groups):
                back = back + msg_ref[group, col, :, :feats]
                tail = tail + msg_ref[group, col, :, feats:]
            pulled = scales_ref[col] * back
            squares = squares + pulled * pulled
        back = msg_ref[0, here, :, :feats]
        for group in range(1, groups):
            back = back + msg_ref[group, here, :, :feats]
        x, r, p = vec_ref[0:1], vec_ref[1:2], vec_ref[2:3]
        q, sp = small_ref[0:1], small_ref[1:2]
        agreement, length = small_ref[2:3, 0:1], small_ref[2:3, 1:2]
        bending = tail[:, width : width + 1] / (n_col * samples)
        curvature = bending + damping * length
        step = agreement / curvature
        product = scale_ref[...] * back / samples + damping * p
        x = x + step * p
        r = r - step * product
        pressed = tail[:, :width] / samples + damping * sp
        q = q - step * pressed
    inv = split(inv_ref[...], 3)
    s = row_dot(stacked_splits(q), inv, NN)
    s0, s1 = s0_ref[...], s1_ref[...]
    z = (r - row_dot(stacked_splits(s), (s0, s1), NN)) / damping
    if first:
        p = z
    else:
        solved = row_dot(stacked_splits(pressed), inv, NN)
        norm = total(squares) / (samples * samples) + 2.0 * damping * bending + damping * damping * length
        bent = (norm - total(pressed * solved)) / damping
        p = z + (step * step * bent / agreement - 1.0) * p
    rounded = (scale_ref[...] * p).astype(jnp.bfloat16)
    ahead = lax.dot_general(
        jnp.broadcast_to(rounded, (8, rounded.shape[1])), design_ref[...], NT,
        preferred_element_type=jnp.float32,
    )[0:1]
    sp = row_dot(stacked_splits(p), (s0, s1), NT)
    scalars = put_scalars((total(r * z), total(p * p)))
    message = jnp.concatenate([ahead, sp, scalars], axis=1)
    for col in range(msg_out.shape[0]):
        msg_out[col] = message
    vec_out[...] = jnp.zeros_like(vec_out)
    vec_out[0:1] = x
    vec_out[1:2] = r
    vec_out[2:3] = p
    small_out[...] = jnp.zeros_like(small_out)
    small_out[0:1] = q


def backward_kernel(last, *refs):
    if last:
        (msg_ref, small_ref, weight_ref, small_out, bend_out) = refs
    else:
        (msg_ref, small_ref, weight_ref, scale_ref, design_ref, s0_ref, s1_ref, small_out, msg_out) = refs
    rows = weight_ref.shape[1]
    width = small_ref.shape[1]
    sums = msg_ref[0]
    for col in range(1, msg_ref.shape[0]):
        sums = sums + msg_ref[col]
    y = sums[:, :rows]
    rest = sums[:, rows + width :]
    inner = (weight_ref[...] * y).astype(jnp.bfloat16)
    bend = total(inner.astype(jnp.float32) * y)
    at = lax.broadcasted_iota(jnp.int32, (1, width), 1)
    small_out[...] = jnp.zeros_like(small_out)
    small_out[0:1] = small_ref[0:1]
    small_out[1:2] = sums[:, rows : rows + width]
    small_out[2:3] = jnp.where(at == 0, rest[:, 0:1], jnp.where(at == 1, rest[:, 1:2], 0.0))
    if last:
        bend_out[...] = put_scalars((bend,))
        return
    back = lax.dot_general(
        jnp.broadcast_to(inner, (8, rows)), design_ref[...], NN, preferred_element_type=jnp.float32
    )[0:1]
    sb = row_dot(stacked_splits(scale_ref[...] * back), (s0_ref[...], s1_ref[...]), NT)
    message = jnp.concatenate([back, sb, put_scalars((bend,))], axis=1)
    for group in range(msg_out.shape[0]):
        for col in range(msg_out.shape[1]):
            msg_out[group, col] = message


def call(kernel, shapes, args, smem=0, flops=4_000_000):
    specs = [pl.BlockSpec(memory_space=pltpu.SMEM)] * smem
    specs += [pl.BlockSpec(memory_space=pltpu.VMEM)] * (len(args) - smem)
    return pl.pallas_call(
        kernel,
        out_shape=[jax.ShapeDtypeStruct(shape, jnp.float32) for shape in shapes],
        in_specs=specs,
        out_specs=[pl.BlockSpec(memory_space=pltpu.VMEM)] * len(shapes),
        cost_estimate=pl.CostEstimate(flops=flops, bytes_accessed=1_000_000, transcendentals=0),
    )(*args)


def heard_cols(row):
    n_col = lax.axis_size("cols")
    return lax.all_to_all(jnp.broadcast_to(row[None], (n_col, *row.shape)), "cols", 0, 0)


def summed_cols(row):
    return jnp.sum(heard_cols(row), 0)


def solve(design, weight, feature_scale, scales, gradient, sketch, inverse, samples):
    n_row, n_col = lax.axis_size("rows"), lax.axis_size("cols")
    rows, feats = design.shape
    width = sketch.shape[0]
    scale = feature_scale[None]
    high = lax.reduce_precision(sketch, 8, 7)
    s0, s1 = high.astype(jnp.bfloat16), (sketch - high).astype(jnp.bfloat16)
    weight = weight[None]
    q = summed_cols(jnp.dot(gradient[None], sketch.T, precision=highest))
    here = lax.axis_index("cols").astype(jnp.int32)[None]
    vec_shape, small_shape = (8, feats), (8, width)
    ahead_shape = (n_col, 1, rows + width + LANES)
    back_shape = (n_row, n_col, 1, feats + width + LANES)
    vec, small, message = call(
        functools.partial(forward_kernel, samples, True),
        (vec_shape, small_shape, ahead_shape),
        (gradient[None], q, scale, design, s0, s1, inverse),
    )
    for turn in range(ITERS):
        message = lax.all_to_all(message, "cols", 0, 0)
        if turn + 1 == ITERS:
            break
        small, message = call(
            functools.partial(backward_kernel, False),
            (small_shape, back_shape),
            (message, small, weight, scale, design, s0, s1),
        )
        message = message.reshape(n_row * n_col, 1, -1)
        message = lax.all_to_all(message, ("rows", "cols"), 0, 0).reshape(back_shape)
        vec, small, message = call(
            functools.partial(forward_kernel, samples, False),
            (vec_shape, small_shape, ahead_shape),
            (here, message, vec, small, scales, scale, design, s0, s1, inverse),
            smem=1,
        )
    small, bend = call(
        functools.partial(backward_kernel, True),
        (small_shape, (1, LANES)),
        (message, small, weight),
    )
    bend = lax.psum(bend, "rows")[0, 0]
    curvature = bend / samples + damping * small[2, 1]
    return vec[0] + small[2, 0] / curvature * vec[2]


def on_device(design, theta, feature_scale, labels, psi, phi):
    row_devices = lax.axis_size("rows")
    samples = design.shape[0] * row_devices
    width = psi.shape[1]
    scaled_theta = (theta * feature_scale).astype(jnp.bfloat16)
    part = jnp.dot(design, scaled_theta, preferred_element_type=jnp.float32)
    rows = part.shape[0]
    heard = heard_cols(jnp.concatenate([part, feature_scale])[None])
    margins = jnp.sum(heard[:, 0, :rows], 0)
    scales = heard[:, :, rows:]
    chance = jax.nn.sigmoid(margins)
    weight = chance * (1.0 - chance)
    misfit = (chance - labels.astype(jnp.float32)).astype(jnp.bfloat16)
    summed_grad = lax.psum(jnp.dot(misfit, design, preferred_element_type=jnp.float32), "rows")
    gradient = feature_scale * summed_grad / samples + damping * theta
    rows_scaled = (
        design.astype(jnp.float32) * jnp.sqrt(weight)[:, None] * feature_scale[None, :]
    ).astype(jnp.bfloat16)
    mixed_cols = jnp.einsum(
        "rf,rs->fs", rows_scaled, psi, preferred_element_type=jnp.float32
    ).astype(jnp.bfloat16)
    range_rows = lax.psum(
        jnp.dot(rows_scaled, mixed_cols, preferred_element_type=jnp.float32), "cols"
    )
    leaf_weights = shrink_weights(range_rows).astype(jnp.bfloat16)
    sketch = jnp.dot(leaf_weights, rows_scaled, preferred_element_type=jnp.float32)
    position = lax.axis_index("rows")
    for level_bit in range(row_devices.bit_length() - 1):
        partner = swapped(sketch, "rows", level_bit)
        first_low = position // (1 << level_bit) % 2 == 0
        lower_half = jnp.where(first_low, sketch, partner)
        upper_half = jnp.where(first_low, partner, sketch)
        stacked = jnp.concatenate([lower_half, upper_half], 0)
        gram = lax.psum(jnp.dot(stacked, stacked.T, precision=highest), "cols")
        range_rows = jnp.dot(gram, phi, precision=highest)
        sketch = jnp.dot(shrink_weights(range_rows), stacked, precision=highest)
    kernel_part = lax.psum(jnp.dot(sketch, sketch.T, precision=highest), "cols")
    kernel = kernel_part + damping * samples * jnp.eye(width, dtype=jnp.float32)
    factor = inverse_factor(kernel, 0.0)
    inverse = jnp.dot(factor.T, factor, precision=highest)
    newton = solve(design, weight, feature_scale, scales, gradient, sketch, inverse, samples)
    return (newton, sketch)


def solution(mesh):
    in_specs = (P("rows", "cols"), P("cols"), P("cols"), P("rows"), P(), P())
    out_specs = (P("cols"), P(None, "cols"))
    return jax.shard_map(
        on_device, mesh=mesh, in_specs=in_specs, out_specs=out_specs, check_vma=False
    )
```

time: 1240 us -> 761 us (0.61)
  blocking collectives: 475 us -> 224 us
  other arithmetic: 259 us -> 9.21 us
  Pallas kernels: 0 us -> 117 us
  matrix products: 123 us -> 47.9 us
  between operations: 48.3 us -> 15.7 us
  local copies, waits for them, and re-layouts: 32.1 us -> 5.36 us
  waiting for transfers between devices: 298 us -> 324 us
    psum x31 -> x1, blocking collectives: 469 us -> 5.87 us  [solve(): bend = lax.psum(bend, 'rows')[0, 0]]
    another operation x46 -> x0, other arithmetic: 223 us -> none  [the longest x20 105 us: shrink_weights(): jnp.linalg.cholesky(moment + ridge * jnp.eye(width, dtype=jnp.float32))]
    all_to_all x0 -> x19, blocking collectives: none -> 212 us  [the longest x9 96.7 us: solve(): message = lax.all_to_all(message, 'cols', 0, 0)]
    pallas_call x0 -> x24, Pallas kernels: none -> 117 us  [the longest x20 75 us: call(): pl.pallas_call(kernel, out_shape=[jax.ShapeDtypeStruct(shape, jnp.float32...]
    dot_general x40 -> x6, matrix products: 52.2 us -> 10.9 us  [the longest x3 5.49 us: shrink_weights(): jnp.dot(inverse_factor(moment, shrink_share), range_rows.T, precision=hig...]
    another operation x77 -> x0, matrix products: 35.6 us -> none  [the longest x60 23.1 us: precondition_plus(): solved = jax.scipy.linalg.cho_solve((kernel_factor, True), projected)]
    reduce_sum x40 -> x1, other arithmetic: 25.6 us -> 0.6 us  [summed_cols(): return jnp.sum(heard_cols(row), 0)]
    another operation x42 -> x0, local copies, waits for them, and re-layouts: 21.7 us -> none  [the longest x13 11.5 us: shrink_weights(): return jax.scipy.linalg.solve_triangular(factor, range_rows.T, lower=True)]
  transfers between devices with their start and end apart: 6 -> 8, of which waited for: 6 -> 8; matrix products, arithmetic and copies ran while one was open for 0% -> 0% of each run, Pallas kernels for 0% -> 0%
where the time goes in v1:
time: 761 us; the launch traced here: 751 us
  waiting for transfers between devices  324 us (43%)
  blocking collectives  224 us (29%)
  Pallas kernels  117 us (15%)
  matrix products  47.9 us (6%)
  between operations  15.7 us (2%)
  other arithmetic  9.21 us (1%)
  starting transfers between devices  8.49 us (1%)
    psum x2, waiting for transfers between devices, on_device(): gram = lax.psum(jnp.dot(stacked, stacked.T, precision=highest), 'cols')  149 us
    all_to_all x9, blocking collectives, solve(): message = lax.all_to_all(message, 'cols', 0, 0)  96.7 us
    all_to_all x8, blocking collectives, solve(): lax.all_to_all(message, ('rows', 'cols'), 0, 0).reshape(back_shape)  90.9 us
    psum x1, waiting for transfers between devices, on_device(): lax.psum(jnp.dot(rows_scaled, mixed_cols, preferred_element_type=jnp.floa...  75.8 us
    pallas_call x20, Pallas kernels, call(): pl.pallas_call(kernel, out_shape=[jax.ShapeDtypeStruct(shape, jnp.float32...  75 us
    psum x1, waiting for transfers between devices, on_device(): kernel_part = lax.psum(jnp.dot(sketch, sketch.T, precision=highest), 'cols')  58.7 us
    pallas_call x4, Pallas kernels, inverse_factor(): pl.pallas_call(functools.partial(factor_kernel, share), out_shape=jax.Sha...  41.6 us
    ppermute x2, waiting for transfers between devices, swapped(): return lax.ppermute(value, axis, pairs)  26.7 us
  transfers between devices with their start and end apart: 8, of which 8 were waited for; matrix products, arithmetic and copies ran while one was open for 0% of the time, Pallas kernels for 0%

profile of v1, /device:TPU:0, one launch (start us, length us, event | category | flops | bytes accessed | tf_op | source)
XLA Modules:
  0.0 751.1 jit_solution(16338981217062154463)
XLA Ops:
  10.4 14.0 %all_to_all.105 = f32[8,1,2048]{2,1,0:T(1,128)S(1)} all-to-all(f32[8,1,2048]{2,1,0:T(1,128)S(1)} %broadcast_in_dim.11), channel_id=1, replica_groups=mesh['rows'=4,'cols'=8] {'cols'}, dimensions={0} | all-to-all | bytes 131072 | tf_op jit(solution)/shard_map/all_to_all | solution.py:245
  28.5 75.8 %all-reduce.5.cloned.1.call-done = f32[1024,256]{1,0:T(8,128)} async-done(((f32[1024,256]{1,0:T(8,128)}), f32[1024,256]{1,0:T(8,128)}) %all-reduce.5.cloned.1.call-update) | async-done | bytes 1048592 | tf_op jit(solution)/shard_map/psum | solution.py:318
  134.2 77.4 %all-reduce.7.cloned.1.call-done = f32[512,512]{1,0:T(8,128)} async-done(((f32[512,512]{1,0:T(8,128)}), f32[512,512]{1,0:T(8,128)}) %all-reduce.7.cloned.1.call-update) | async-done | bytes 1048592 | tf_op jit(solution)/shard_map/psum | solution.py:330
  233.5 23.7 %collective-permute-done.1 = f32[256,1024]{1,0:T(8,128)} collective-permute-done((f32[256,1024]{1,0:T(8,128)}, f32[256,1024]{1,0:T(8,128)}, u32[]{:S(2)}, u32[]{:S(2)}) %collective-permute-start.1) | collective-permute-done | bytes 1048608 | tf_op jit(solution)/shard_map/ppermute | solution.py:26
  271.1 71.2 %all-reduce.9.cloned.1.call-done = f32[512,512]{1,0:T(8,128)} async-done(((f32[512,512]{1,0:T(8,128)}), f32[512,512]{1,0:T(8,128)}) %all-reduce.9.cloned.1.call-update) | async-done | bytes 1048592 | tf_op jit(solution)/shard_map/psum | solution.py:330
  365.0 10.5 %all_to_all.106 = f32[8,1,256]{2,1,0:T(1,128)S(1)} all-to-all(f32[8,1,256]{2,1,0:T(1,128)S(1)} %broadcast_in_dim.13), channel_id=1, replica_groups=mesh['rows'=4,'cols'=8] {'cols'}, dimensions={0} | all-to-all | bytes 16384 | tf_op jit(solution)/shard_map/all_to_all | solution.py:245
  376.1 58.7 %all-reduce.11.cloned.1.call-done = f32[256,256]{1,0:T(8,128)} async-done(((f32[256,256]{1,0:T(8,128)}), f32[256,256]{1,0:T(8,128)}) %all-reduce.11.cloned.1.call-update) | async-done | bytes 262160 | tf_op jit(solution)/shard_map/psum | solution.py:333
  483.4 10.7 %all_to_all.107.refs_0_ = f32[8,1,1408]{2,1,0:T(1,128)} all-to-all(f32[8,1,1408]{2,1,0:T(1,128)} %get-tuple-element.57), channel_id=1, replica_groups=mesh['rows'=4,'cols'=8] {'cols'}, dimensions={0} | all-to-all | bytes 90112 | tf_op jit(solution)/shard_map/all_to_all | solution.py:271
  497.5 11.5 %all_to_all.108 = f32[32,1,1408]{2,1,0:T(1,128)} all-to-all(f32[32,1,1408]{2,1,0:T(1,128)} %bitcast.89), channel_id=1, replica_groups=mesh['rows'=4,'cols'=8] {'rows','cols'}, dimensions={0} | all-to-all | bytes 360448 | tf_op jit(solution)/shard_map/all_to_all | solution.py:280
  513.4 10.7 %all_to_all.109.refs_0_ = f32[8,1,1408]{2,1,0:T(1,128)} all-to-all(f32[8,1,1408]{2,1,0:T(1,128)} %get-tuple-element.62), channel_id=1, replica_groups=mesh['rows'=4,'cols'=8] {'cols'}, dimensions={0} | all-to-all | bytes 90112 | tf_op jit(solution)/shard_map/all_to_all | solution.py:271
  527.5 11.3 %all_to_all.110 = f32[32,1,1408]{2,1,0:T(1,128)} all-to-all(f32[32,1,1408]{2,1,0:T(1,128)} %bitcast.90), channel_id=1, replica_groups=mesh['rows'=4,'cols'=8] {'rows','cols'}, dimensions={0} | all-to-all | bytes 360448 | tf_op jit(solution)/shard_map/all_to_all | solution.py:280
  543.2 10.7 %all_to_all.111.refs_0_ = f32[8,1,1408]{2,1,0:T(1,128)} all-to-all(f32[8,1,1408]{2,1,0:T(1,128)} %get-tuple-element.67), channel_id=1, replica_groups=mesh['rows'=4,'cols'=8] {'cols'}, dimensions={0} | all-to-all | bytes 90112 | tf_op jit(solution)/shard_map/all_to_all | solution.py:271
  557.3 11.3 %all_to_all.112 = f32[32,1,1408]{2,1,0:T(1,128)} all-to-all(f32[32,1,1408]{2,1,0:T(1,128)} %bitcast.91), channel_id=1, replica_groups=mesh['rows'=4,'cols'=8] {'rows','cols'}, dimensions={0} | all-to-all | bytes 360448 | tf_op jit(solution)/shard_map/all_to_all | solution.py:280
  573.1 10.7 %all_to_all.113.refs_0_ = f32[8,1,1408]{2,1,0:T(1,128)} all-to-all(f32[8,1,1408]{2,1,0:T(1,128)} %get-tuple-element.72), channel_id=1, replica_groups=mesh['rows'=4,'cols'=8] {'cols'}, dimensions={0} | all-to-all | bytes 90112 | tf_op jit(solution)/shard_map/all_to_all | solution.py:271
  587.1 11.3 %all_to_all.114 = f32[32,1,1408]{2,1,0:T(1,128)} all-to-all(f32[32,1,1408]{2,1,0:T(1,128)} %bitcast.92), channel_id=1, replica_groups=mesh['rows'=4,'cols'=8] {'rows','cols'}, dimensions={0} | all-to-all | bytes 360448 | tf_op jit(solution)/shard_map/all_to_all | solution.py:280
  602.9 10.7 %all_to_all.115.refs_0_ = f32[8,1,1408]{2,1,0:T(1,128)} all-to-all(f32[8,1,1408]{2,1,0:T(1,128)} %get-tuple-element.77), channel_id=1, replica_groups=mesh['rows'=4,'cols'=8] {'cols'}, dimensions={0} | all-to-all | bytes 90112 | tf_op jit(solution)/shard_map/all_to_all | solution.py:271
  616.9 11.3 %all_to_all.116 = f32[32,1,1408]{2,1,0:T(1,128)} all-to-all(f32[32,1,1408]{2,1,0:T(1,128)} %bitcast.93), channel_id=1, replica_groups=mesh['rows'=4,'cols'=8] {'rows','cols'}, dimensions={0} | all-to-all | bytes 360448 | tf_op jit(solution)/shard_map/all_to_all | solution.py:280
  632.7 10.7 %all_to_all.117.refs_0_ = f32[8,1,1408]{2,1,0:T(1,128)} all-to-all(f32[8,1,1408]{2,1,0:T(1,128)} %get-tuple-element.82), channel_id=1, replica_groups=mesh['rows'=4,'cols'=8] {'cols'}, dimensions={0} | all-to-all | bytes 90112 | tf_op jit(solution)/shard_map/all_to_all | solution.py:271
  646.7 11.3 %all_to_all.118 = f32[32,1,1408]{2,1,0:T(1,128)} all-to-all(f32[32,1,1408]{2,1,0:T(1,128)} %bitcast.94), channel_id=1, replica_groups=mesh['rows'=4,'cols'=8] {'rows','cols'}, dimensions={0} | all-to-all | bytes 360448 | tf_op jit(solution)/shard_map/all_to_all | solution.py:280
  662.5 10.7 %all_to_all.119.refs_0_ = f32[8,1,1408]{2,1,0:T(1,128)} all-to-all(f32[8,1,1408]{2,1,0:T(1,128)} %get-tuple-element.87), channel_id=1, replica_groups=mesh['rows'=4,'cols'=8] {'cols'}, dimensions={0} | all-to-all | bytes 90112 | tf_op jit(solution)/shard_map/all_to_all | solution.py:271
  676.5 11.3 %all_to_all.120 = f32[32,1,1408]{2,1,0:T(1,128)} all-to-all(f32[32,1,1408]{2,1,0:T(1,128)} %bitcast.95), channel_id=1, replica_groups=mesh['rows'=4,'cols'=8] {'rows','cols'}, dimensions={0} | all-to-all | bytes 360448 | tf_op jit(solution)/shard_map/all_to_all | solution.py:280
  692.3 10.7 %all_to_all.121.refs_0_ = f32[8,1,1408]{2,1,0:T(1,128)} all-to-all(f32[8,1,1408]{2,1,0:T(1,128)} %get-tuple-element.92), channel_id=1, replica_groups=mesh['rows'=4,'cols'=8] {'cols'}, dimensions={0} | all-to-all | bytes 90112 | tf_op jit(solution)/shard_map/all_to_all | solution.py:271
  706.3 11.3 %all_to_all.122 = f32[32,1,1408]{2,1,0:T(1,128)} all-to-all(f32[32,1,1408]{2,1,0:T(1,128)} %bitcast.96), channel_id=1, replica_groups=mesh['rows'=4,'cols'=8] {'rows','cols'}, dimensions={0} | all-to-all | bytes 360448 | tf_op jit(solution)/shard_map/all_to_all | solution.py:280
  722.1 10.7 %all_to_all.123.refs_0_ = f32[8,1,1408]{2,1,0:T(1,128)} all-to-all(f32[8,1,1408]{2,1,0:T(1,128)} %get-tuple-element.98), channel_id=1, replica_groups=mesh['rows'=4,'cols'=8] {'cols'}, dimensions={0} | all-to-all | bytes 90112 | tf_op jit(solution)/shard_map/all_to_all | solution.py:271
  (106 shorter events, 216.5 us)
Async XLA Ops:
  7.2 17.9 %copy-start = (bf16[1024,256]{1,0:T(8,128)(2,1)S(1)}, bf16[1024,256]{1,0:T(8,128)(2,1)}, u32[]{:S(2)}) copy-start(bf16[1024,256]{1,0:T(8,128)(2,1)} %param.10) | copy-start | bytes 1572868
  7.2 3.2 copy-start.9
  7.2 17.9 %copy-start.1 = (bf16[1024,1024]{1,0:T(8,128)(2,1)S(1)}, bf16[1024,1024]{1,0:T(8,128)(2,1)}, u32[]{:S(2)}) copy-start(bf16[1024,1024]{1,0:T(8,128)(2,1)} %refs_6_.17) | copy-start | bytes 6291460
  7.2 17.8 %copy-start.14 = (s32[1024]{0:T(1024)S(1)}, s32[1024]{0:T(1024)}, u32[]{:S(2)}) copy-start(s32[1024]{0:T(1024)} %param.9) | copy-start | bytes 12292
  7.2 97.1 %all-reduce.5.cloned.1.call-start = ((), (), s32[]{:S(2)}) async-start(), calls=%async_computation.21 | async-start | bytes 2097152 | tf_op jit(solution)/shard_map/psum | solution.py:318
  28.5 183.1 %all-reduce.7.cloned.1.call-start = ((), (), s32[]{:S(2)}) async-start(), calls=%async_computation.22 | async-start | bytes 2097152 | tf_op jit(solution)/shard_map/psum | solution.py:330
  123.1 3.0 collective-permute-start
  127.8 1.0 copy-start.3
  127.8 1.3 copy-start.4
  133.6 208.6 %all-reduce.9.cloned.1.call-start = ((), (), s32[]{:S(2)}) async-start(), calls=%async_computation.23 | async-start | bytes 2097152 | tf_op jit(solution)/shard_map/psum | solution.py:330
  232.0 25.2 %collective-permute-start.1 = (f32[256,1024]{1,0:T(8,128)}, f32[256,1024]{1,0:T(8,128)}, u32[]{:S(2)}, u32[]{:S(2)}) collective-permute-start(f32[256,1024]{1,0:T(8,128)} %fusion.2), channel_id=1, source_target_pairs={{0,16},{8,24},{16,0},{24,8},{1,17},{9,25},{17,1},{25,9},{2,18},{10... | collective-permute-start | bytes 3145736 | tf_op jit(solution)/shard_map/ppermute | solution.py:26
  258.9 1.0 copy-start.5
  258.9 1.3 copy-start.7
  264.7 6.3 copy-start.13
  264.7 77.5 %copy-start.8 = (f32[512,256]{1,0:T(8,128)S(1)}, f32[512,256]{1,0:T(8,128)}, u32[]{:S(2)}) copy-start(f32[512,256]{1,0:T(8,128)} %param.11) | copy-start | bytes 1572868
  264.8 170.0 %all-reduce.11.cloned.1.call-start = ((), (), s32[]{:S(2)}) async-start(), calls=%async_computation.24 | async-start | bytes 524288 | tf_op jit(solution)/shard_map/psum | solution.py:333
  271.0 93.0 %copy-start.12 = (f32[1024]{0:T(1024)}, f32[1024]{0:T(1024)S(1)}, u32[]{:S(2)}) copy-start(f32[1024]{0:T(1024)S(1)} %multiply_add_fusion.1) | copy-start | bytes 12292
  271.1 87.1 %copy-start.6 = (f32[256,1024]{1,0:T(8,128)S(1)}, f32[256,1024]{1,0:T(8,128)}, u32[]{:S(2)}) copy-start(f32[256,1024]{1,0:T(8,128)} %copy-done.5) | copy-start | bytes 3145732
  362.3 74.2 %copy-start.2 = (f32[256,1024]{1,0:T(8,128)}, f32[256,1024]{1,0:T(8,128)S(1)}, u32[]{:S(2)}) copy-start(f32[256,1024]{1,0:T(8,128)S(1)} %get-tuple-element.115) | copy-start | bytes 3145732
  453.2 10.6 %all-to-all-start.2 = ((f32[8,1,1408]{2,1,0:T(1,128)}), f32[8,1,1408]{2,1,0:T(1,128)S(1)}, u32[]{:S(2)}, u32[]{:S(2)}) async-start(f32[8,1,1408]{2,1,0:T(1,128)} %get-tuple-element.52), calls=%async_computation.2 | async-start | bytes 90112 | tf_op jit(solution)/shard_map/all_to_all | solution.py:271
  463.8 0.6 copy-start.11
  467.7 10.7 %all-to-all-start.3 = ((f32[32,1,1408]{2,1,0:T(1,128)}), f32[32,1,1408]{2,1,0:T(1,128)S(1)}, u32[]{:S(2)}, u32[]{:S(2)}) async-start(f32[32,1,1408]{2,1,0:T(1,128)} %bitcast.88), calls=%async_computation.3 | async-start | bytes 360448 | tf_op jit(solution)/shard_map/all_to_all | solution.py:280
  478.4 0.7 copy-start.10
Sparse Core Ops, SparseCore 0:
  28.6 75.6 all-reduce.4
  133.8 77.7 all-reduce.6
  264.9 77.2 all-reduce.8
  364.1 70.6 all-reduce.10

commit v2 on v1

--- a/solution.py
+++ b/solution.py
@@ -15,6 +15,7 @@
 highest = lax.Precision.HIGHEST
 LANES = 128
 BLOCK = 16
+VMEM_LIMIT = 16 * 1024 * 1024
 NT = (((1,), (1,)), ((), ()))
 NN = (((1,), (0,)), ((), ()))
 TN = (((0,), (0,)), ((), ()))
@@ -29,6 +30,64 @@
 def shrink_weights(range_rows):
     moment = jnp.dot(range_rows.T, range_rows, precision=highest)
     return jnp.dot(inverse_factor(moment, shrink_share), range_rows.T, precision=highest)
+
+
+def scattered_cols(part):
+    n_col = lax.axis_size("cols")
+    blocks = part.reshape(n_col, part.shape[0] // n_col, part.shape[1])
+    return jnp.sum(lax.all_to_all(blocks, "cols", 0, 0), 0)
+
+
+def summed_blocks(part):
+    n_col = lax.axis_size("cols")
+    block = scattered_cols(part)
+    sent = jnp.broadcast_to(block[None], (n_col, *block.shape))
+    return lax.all_to_all(sent, "cols", 0, 0).reshape(part.shape)
+
+
+def in_order(first, mine, other):
+    return jnp.where(first, mine, other), jnp.where(first, other, mine)
+
+
+def rows_at(value, index, count):
+    size = value.shape[0] // count
+    return lax.dynamic_slice_in_dim(value, index * size, size, 0)
+
+
+def leaf_gram(leaf, position):
+    width = leaf.shape[0]
+    low = position % 2 == 0
+    lower, upper = in_order(low, leaf, swapped(leaf, "rows", 0))
+    piece = rows_at(lower, position % 2, 2)
+    share = jnp.concatenate([gram_of(leaf, leaf), gram_of(piece, upper)], 0)
+    share = summed_blocks(share)
+    first, second = in_order(low, share, swapped(share, "rows", 0))
+    cross = jnp.concatenate([first[width:], second[width:]], 0)
+    return jnp.concatenate([lower, upper], 0), first[:width], second[:width], cross
+
+
+def gram_of(left, right):
+    return lax.dot_general(left, right, NT, precision=highest)
+
+
+def merge_gram(sketch, gram, position, level):
+    n_row, n_col = lax.axis_size("rows"), lax.axis_size("cols")
+    width, feats = sketch.shape
+    group = 1 << level
+    both = jnp.concatenate([rows_at(sketch, position % group, group), rows_at(gram, position % group, group)], 1)
+    both = swapped(both, "rows", level)
+    for bit in range(level):
+        first, second = in_order(position // (1 << bit) % 2 == 0, both, swapped(both, "rows", bit))
+        both = jnp.concatenate([first, second], 0)
+    low = position // group % 2 == 0
+    lower, upper = in_order(low, sketch, both[:, :feats])
+    first, second = in_order(low, gram, both[:, feats:])
+    part = gram_of(rows_at(lower, position % (2 * group), 2 * group), upper)
+    block = scattered_cols(part)
+    sent = jnp.broadcast_to(block[None], (n_row * n_col, *block.shape))
+    heard = lax.all_to_all(sent, ("rows", "cols"), 0, 0).reshape(n_row, -1, width)
+    cross = lax.dynamic_slice_in_dim(heard, position // (2 * group) * (2 * group), 2 * group, 0)
+    return jnp.concatenate([lower, upper], 0), first, second, cross.reshape(width, width)
 
 
 def split(value, parts):
@@ -96,6 +155,7 @@
         in_specs=[pl.BlockSpec(memory_space=pltpu.VMEM)],
         out_specs=pl.BlockSpec(memory_space=pltpu.VMEM),
         scratch_shapes=[pltpu.VMEM((n, n), jnp.float32)],
+        compiler_params=pltpu.CompilerParams(vmem_limit_bytes=VMEM_LIMIT),
         cost_estimate=pl.CostEstimate(flops=20_000_000, bytes_accessed=600_000, transcendentals=0),
     )(m)
 
@@ -236,6 +296,7 @@
         out_shape=[jax.ShapeDtypeStruct(shape, jnp.float32) for shape in shapes],
         in_specs=specs,
         out_specs=[pl.BlockSpec(memory_space=pltpu.VMEM)] * len(shapes),
+        compiler_params=pltpu.CompilerParams(vmem_limit_bytes=VMEM_LIMIT),
         cost_estimate=pl.CostEstimate(flops=flops, bytes_accessed=1_000_000, transcendentals=0),
     )(*args)
 
@@ -249,7 +310,7 @@
     return jnp.sum(heard_cols(row), 0)
 
 
-def solve(design, weight, feature_scale, scales, gradient, sketch, inverse, samples):
+def solve(design, weight, feature_scale, scales, gradient, sketch, q, inverse, samples):
     n_row, n_col = lax.axis_size("rows"), lax.axis_size("cols")
     rows, feats = design.shape
     width = sketch.shape[0]
@@ -257,7 +318,6 @@
     high = lax.reduce_precision(sketch, 8, 7)
     s0, s1 = high.astype(jnp.bfloat16), (sketch - high).astype(jnp.bfloat16)
     weight = weight[None]
-    q = summed_cols(jnp.dot(gradient[None], sketch.T, precision=highest))
     here = lax.axis_index("cols").astype(jnp.int32)[None]
     vec_shape, small_shape = (8, feats), (8, width)
     ahead_shape = (n_col, 1, rows + width + LANES)
@@ -315,26 +375,29 @@
     mixed_cols = jnp.einsum(
         "rf,rs->fs", rows_scaled, psi, preferred_element_type=jnp.float32
     ).astype(jnp.bfloat16)
-    range_rows = lax.psum(
-        jnp.dot(rows_scaled, mixed_cols, preferred_element_type=jnp.float32), "cols"
+    range_rows = summed_blocks(
+        jnp.dot(rows_scaled, mixed_cols, preferred_element_type=jnp.float32)
     )
     leaf_weights = shrink_weights(range_rows).astype(jnp.bfloat16)
     sketch = jnp.dot(leaf_weights, rows_scaled, preferred_element_type=jnp.float32)
     position = lax.axis_index("rows")
-    for level_bit in range(row_devices.bit_length() - 1):
-        partner = swapped(sketch, "rows", level_bit)
-        first_low = position // (1 << level_bit) % 2 == 0
-        lower_half = jnp.where(first_low, sketch, partner)
-        upper_half = jnp.where(first_low, partner, sketch)
-        stacked = jnp.concatenate([lower_half, upper_half], 0)
-        gram = lax.psum(jnp.dot(stacked, stacked.T, precision=highest), "cols")
-        range_rows = jnp.dot(gram, phi, precision=highest)
-        sketch = jnp.dot(shrink_weights(range_rows), stacked, precision=highest)
-    kernel_part = lax.psum(jnp.dot(sketch, sketch.T, precision=highest), "cols")
-    kernel = kernel_part + damping * samples * jnp.eye(width, dtype=jnp.float32)
+    for level in range(row_devices.bit_length() - 1):
+        if level == 0:
+            stacked, first, second, cross = leaf_gram(sketch, position)
+        else:
+            stacked, first, second, cross = merge_gram(sketch, gram, position, level)
+        full = jnp.concatenate(
+            [jnp.concatenate([first, cross], 1), jnp.concatenate([cross.T, second], 1)], 0
+        )
+        weights = shrink_weights(jnp.dot(full, phi, precision=highest))
+        sketch = jnp.dot(weights, stacked, precision=lax.Precision.HIGH)
+        gram = gram_of(jnp.dot(weights, full, precision=highest), weights)
+    felt = summed_cols(gram_of(gradient[None], stacked))
+    q = gram_of(felt, weights)
+    kernel = gram + damping * samples * jnp.eye(width, dtype=jnp.float32)
     factor = inverse_factor(kernel, 0.0)
     inverse = jnp.dot(factor.T, factor, precision=highest)
-    newton = solve(design, weight, feature_scale, scales, gradient, sketch, inverse, samples)
+    newton = solve(design, weight, feature_scale, scales, gradient, sketch, q, inverse, samples)
     return (newton, sketch)
 
 

time: 761 us -> 485 us (0.64)
  waiting for transfers between devices: 324 us -> 50.6 us
  blocking collectives: 224 us -> 288 us
  Pallas kernels: 117 us -> 60.8 us
  between operations: 15.7 us -> 3.12 us
  matrix products: 47.9 us -> 36 us
  starting transfers between devices: 8.49 us -> 18.3 us
    psum x4 -> x0, waiting for transfers between devices: 283 us -> none  [the longest x2 149 us: on_device(): gram = lax.psum(jnp.dot(stacked, stacked.T, precision=highest), 'cols')]
    all_to_all x0 -> x4, blocking collectives: none -> 88.6 us  [the longest x2 44.7 us: scattered_cols(): return jnp.sum(lax.all_to_all(blocks, 'cols', 0, 0), 0)]
    pallas_call x20, Pallas kernels: 75 us -> 25.8 us  [call(): pl.pallas_call(kernel, out_shape=[jax.ShapeDtypeStruct(shape, jnp.float32...]
    all_to_all x0 -> x3, waiting for transfers between devices: none -> 18.5 us  [the longest x1 8.54 us: merge_gram(): lax.all_to_all(sent, ('rows', 'cols'), 0, 0).reshape(n_row, -1, width)]
    all_to_all x8, blocking collectives: 90.9 us -> 78.2 us  [solve(): lax.all_to_all(message, ('rows', 'cols'), 0, 0).reshape(back_shape)]
    all_to_all x2 -> x1, blocking collectives: 24.5 us -> 14 us  [heard_cols(): lax.all_to_all(jnp.broadcast_to(row[None], (n_col, *row.shape)), 'cols',...]
    all_to_all x0 -> x3, starting transfers between devices: none -> 10.2 us  [the longest x1 3.52 us: merge_gram(): lax.all_to_all(sent, ('rows', 'cols'), 0, 0).reshape(n_row, -1, width)]
    ppermute x2 -> x4, waiting for transfers between devices: 26.7 us -> 17.3 us  [swapped(): return lax.ppermute(value, axis, pairs)]
  transfers between devices with their start and end apart: 8 -> 9, of which waited for: 8 -> 8; matrix products, arithmetic and copies ran while one was open for 0% -> 2% of each run, Pallas kernels for 0% -> 0%
where the time goes in v2:
time: 485 us; the launch traced here: 476 us
  blocking collectives  288 us (59%)
  Pallas kernels  60.8 us (13%)
  waiting for transfers between devices  50.6 us (10%)
  matrix products  36 us (7%)
  starting transfers between devices  18.3 us (4%)
  local copies, waits for them, and re-layouts  11.1 us (2%)
  other arithmetic  8.31 us (2%)
    all_to_all x9, blocking collectives, solve(): message = lax.all_to_all(message, 'cols', 0, 0)  94.2 us
    all_to_all x8, blocking collectives, solve(): lax.all_to_all(message, ('rows', 'cols'), 0, 0).reshape(back_shape)  78.2 us
    all_to_all x2, blocking collectives, scattered_cols(): return jnp.sum(lax.all_to_all(blocks, 'cols', 0, 0), 0)  44.7 us
    all_to_all x2, blocking collectives, summed_blocks(): return lax.all_to_all(sent, 'cols', 0, 0).reshape(part.shape)  43.9 us
    pallas_call x4, Pallas kernels, inverse_factor(): pl.pallas_call(functools.partial(factor_kernel, share), out_shape=jax.Sha...  35 us
    pallas_call x20, Pallas kernels, call(): pl.pallas_call(kernel, out_shape=[jax.ShapeDtypeStruct(shape, jnp.float32...  25.8 us
    ppermute x4, waiting for transfers between devices, swapped(): return lax.ppermute(value, axis, pairs)  17.3 us
    all_to_all x1, blocking collectives, heard_cols(): lax.all_to_all(jnp.broadcast_to(row[None], (n_col, *row.shape)), 'cols',...  14 us
  transfers between devices with their start and end apart: 9, of which 8 were waited for; matrix products, arithmetic and copies ran while one was open for 2% of the time, Pallas kernels for 0%

profile of v2, /device:TPU:0, one launch (start us, length us, event | category | flops | bytes accessed | tf_op | source)
XLA Modules:
  0.0 476.0 jit_solution(1809284187198233447)
XLA Ops:
  3.8 14.0 %all_to_all.135 = f32[8,1,2048]{2,1,0:T(1,128)S(1)} all-to-all(f32[8,1,2048]{2,1,0:T(1,128)S(1)} %broadcast_in_dim.17), channel_id=1, replica_groups=mesh['rows'=4,'cols'=8] {'cols'}, dimensions={0} | all-to-all | bytes 131072 | tf_op jit(solution)/shard_map/all_to_all | solution.py:306
  21.3 28.9 %all_to_all.136 = f32[8,128,256]{2,1,0:T(8,128)} all-to-all(f32[8,128,256]{2,1,0:T(8,128)} %bitcast.124), channel_id=1, replica_groups=mesh['rows'=4,'cols'=8] {'cols'}, dimensions={0} | all-to-all | bytes 2097152 | tf_op jit(solution)/shard_map/all_to_all | solution.py:38
  51.6 28.7 %all_to_all.137 = f32[8,128,256]{2,1,0:T(8,128)S(1)} all-to-all(f32[8,128,256]{2,1,0:T(8,128)S(1)} %broadcast_in_dim.19), channel_id=1, replica_groups=mesh['rows'=4,'cols'=8] {'cols'}, dimensions={0} | all-to-all | bytes 2097152 | tf_op jit(solution)/shard_map/all_to_all | solution.py:45
  100.8 15.8 %all_to_all.138 = f32[8,48,256]{2,1,0:T(8,128)S(1)} all-to-all(f32[8,48,256]{2,1,0:T(8,128)S(1)} %bitcast.122), channel_id=1, replica_groups=mesh['rows'=4,'cols'=8] {'cols'}, dimensions={0} | all-to-all | bytes 786432 | tf_op jit(solution)/shard_map/all_to_all | solution.py:38
  116.7 15.2 %all_to_all.139 = f32[8,48,256]{2,1,0:T(8,128)S(1)} all-to-all(f32[8,48,256]{2,1,0:T(8,128)S(1)} %broadcast_in_dim.20), channel_id=1, replica_groups=mesh['rows'=4,'cols'=8] {'cols'}, dimensions={0} | all-to-all | bytes 786432 | tf_op jit(solution)/shard_map/all_to_all | solution.py:45
  153.0 15.3 %collective-permute-done.2 = f32[128,1280]{1,0:T(8,128)S(1)} collective-permute-done((f32[128,1280]{1,0:T(8,128)S(1)}, f32[128,1280]{1,0:T(8,128)S(1)}, u32[]{:S(2)}, u32[]{:S(2)}) %collective-permute-start.2) | collective-permute-done | bytes 655392 | tf_op jit(solution)/shard_map/ppermute | solution.py:27
  235.7 8.8 %shard_map.80 = f32[256,256]{1,0:T(8,128)S(1)} custom-call(f32[256,256]{1,0:T(8,128)S(1)} %convolution_add_fusion.m_ref), custom_call_target="tpu_custom_call" | custom-call | flops 20000000 | bytes 600000 | tf_op jit(solution)/shard_map/pallas_call | solution.py:152
  274.7 10.4 %all_to_all.140.refs_0_ = f32[8,1,1408]{2,1,0:T(1,128)S(1)} all-to-all(f32[8,1,1408]{2,1,0:T(1,128)S(1)} %get-tuple-element.57), channel_id=1, replica_groups=mesh['rows'=4,'cols'=8] {'cols'}, dimensions={0} | all-to-all | bytes 90112 | tf_op jit(solution)/shard_map/all_to_all | solution.py:331
  285.9 9.8 %all_to_all.141 = f32[32,1,1408]{2,1,0:T(1,128)S(1)} all-to-all(f32[32,1,1408]{2,1,0:T(1,128)S(1)} %bitcast.111), channel_id=1, replica_groups=mesh['rows'=4,'cols'=8] {'rows','cols'}, dimensions={0} | all-to-all | bytes 360448 | tf_op jit(solution)/shard_map/all_to_all | solution.py:340
  297.5 10.7 %all_to_all.142.refs_0_ = f32[8,1,1408]{2,1,0:T(1,128)S(1)} all-to-all(f32[8,1,1408]{2,1,0:T(1,128)S(1)} %get-tuple-element.62), channel_id=1, replica_groups=mesh['rows'=4,'cols'=8] {'cols'}, dimensions={0} | all-to-all | bytes 90112 | tf_op jit(solution)/shard_map/all_to_all | solution.py:331
  308.9 9.8 %all_to_all.143 = f32[32,1,1408]{2,1,0:T(1,128)S(1)} all-to-all(f32[32,1,1408]{2,1,0:T(1,128)S(1)} %bitcast.112), channel_id=1, replica_groups=mesh['rows'=4,'cols'=8] {'rows','cols'}, dimensions={0} | all-to-all | bytes 360448 | tf_op jit(solution)/shard_map/all_to_all | solution.py:340
  320.5 10.4 %all_to_all.144.refs_0_ = f32[8,1,1408]{2,1,0:T(1,128)S(1)} all-to-all(f32[8,1,1408]{2,1,0:T(1,128)S(1)} %get-tuple-element.67), channel_id=1, replica_groups=mesh['rows'=4,'cols'=8] {'cols'}, dimensions={0} | all-to-all | bytes 90112 | tf_op jit(solution)/shard_map/all_to_all | solution.py:331
  331.7 9.8 %all_to_all.145 = f32[32,1,1408]{2,1,0:T(1,128)S(1)} all-to-all(f32[32,1,1408]{2,1,0:T(1,128)S(1)} %bitcast.113), channel_id=1, replica_groups=mesh['rows'=4,'cols'=8] {'rows','cols'}, dimensions={0} | all-to-all | bytes 360448 | tf_op jit(solution)/shard_map/all_to_all | solution.py:340
  343.2 10.4 %all_to_all.146.refs_0_ = f32[8,1,1408]{2,1,0:T(1,128)S(1)} all-to-all(f32[8,1,1408]{2,1,0:T(1,128)S(1)} %get-tuple-element.72), channel_id=1, replica_groups=mesh['rows'=4,'cols'=8] {'cols'}, dimensions={0} | all-to-all | bytes 90112 | tf_op jit(solution)/shard_map/all_to_all | solution.py:331
  354.4 9.8 %all_to_all.147 = f32[32,1,1408]{2,1,0:T(1,128)S(1)} all-to-all(f32[32,1,1408]{2,1,0:T(1,128)S(1)} %bitcast.114), channel_id=1, replica_groups=mesh['rows'=4,'cols'=8] {'rows','cols'}, dimensions={0} | all-to-all | bytes 360448 | tf_op jit(solution)/shard_map/all_to_all | solution.py:340
  366.0 10.4 %all_to_all.148.refs_0_ = f32[8,1,1408]{2,1,0:T(1,128)S(1)} all-to-all(f32[8,1,1408]{2,1,0:T(1,128)S(1)} %get-tuple-element.77), channel_id=1, replica_groups=mesh['rows'=4,'cols'=8] {'cols'}, dimensions={0} | all-to-all | bytes 90112 | tf_op jit(solution)/shard_map/all_to_all | solution.py:331
  377.2 9.8 %all_to_all.149 = f32[32,1,1408]{2,1,0:T(1,128)S(1)} all-to-all(f32[32,1,1408]{2,1,0:T(1,128)S(1)} %bitcast.115), channel_id=1, replica_groups=mesh['rows'=4,'cols'=8] {'rows','cols'}, dimensions={0} | all-to-all | bytes 360448 | tf_op jit(solution)/shard_map/all_to_all | solution.py:340
  388.7 10.4 %all_to_all.150.refs_0_ = f32[8,1,1408]{2,1,0:T(1,128)S(1)} all-to-all(f32[8,1,1408]{2,1,0:T(1,128)S(1)} %get-tuple-element.82), channel_id=1, replica_groups=mesh['rows'=4,'cols'=8] {'cols'}, dimensions={0} | all-to-all | bytes 90112 | tf_op jit(solution)/shard_map/all_to_all | solution.py:331
  399.9 9.8 %all_to_all.151 = f32[32,1,1408]{2,1,0:T(1,128)S(1)} all-to-all(f32[32,1,1408]{2,1,0:T(1,128)S(1)} %bitcast.116), channel_id=1, replica_groups=mesh['rows'=4,'cols'=8] {'rows','cols'}, dimensions={0} | all-to-all | bytes 360448 | tf_op jit(solution)/shard_map/all_to_all | solution.py:340
  411.5 10.4 %all_to_all.152.refs_0_ = f32[8,1,1408]{2,1,0:T(1,128)S(1)} all-to-all(f32[8,1,1408]{2,1,0:T(1,128)S(1)} %get-tuple-element.87), channel_id=1, replica_groups=mesh['rows'=4,'cols'=8] {'cols'}, dimensions={0} | all-to-all | bytes 90112 | tf_op jit(solution)/shard_map/all_to_all | solution.py:331
  422.7 9.8 %all_to_all.153 = f32[32,1,1408]{2,1,0:T(1,128)S(1)} all-to-all(f32[32,1,1408]{2,1,0:T(1,128)S(1)} %bitcast.117), channel_id=1, replica_groups=mesh['rows'=4,'cols'=8] {'rows','cols'}, dimensions={0} | all-to-all | bytes 360448 | tf_op jit(solution)/shard_map/all_to_all | solution.py:340
  434.2 10.4 %all_to_all.154.refs_0_ = f32[8,1,1408]{2,1,0:T(1,128)S(1)} all-to-all(f32[8,1,1408]{2,1,0:T(1,128)S(1)} %get-tuple-element.92), channel_id=1, replica_groups=mesh['rows'=4,'cols'=8] {'cols'}, dimensions={0} | all-to-all | bytes 90112 | tf_op jit(solution)/shard_map/all_to_all | solution.py:331
  445.4 9.8 %all_to_all.155 = f32[32,1,1408]{2,1,0:T(1,128)S(1)} all-to-all(f32[32,1,1408]{2,1,0:T(1,128)S(1)} %bitcast.118), channel_id=1, replica_groups=mesh['rows'=4,'cols'=8] {'rows','cols'}, dimensions={0} | all-to-all | bytes 360448 | tf_op jit(solution)/shard_map/all_to_all | solution.py:340
  457.0 10.4 %all_to_all.156.refs_0_ = f32[8,1,1408]{2,1,0:T(1,128)S(1)} all-to-all(f32[8,1,1408]{2,1,0:T(1,128)S(1)} %get-tuple-element.98), channel_id=1, replica_groups=mesh['rows'=4,'cols'=8] {'cols'}, dimensions={0} | all-to-all | bytes 90112 | tf_op jit(solution)/shard_map/all_to_all | solution.py:331
  (154 shorter events, 173.9 us)
Async XLA Ops:
  0.6 17.3 %copy-start = (bf16[1024,256]{1,0:T(8,128)(2,1)S(1)}, bf16[1024,256]{1,0:T(8,128)(2,1)}, u32[]{:S(2)}) copy-start(bf16[1024,256]{1,0:T(8,128)(2,1)} %param.10) | copy-start | bytes 1572868
  0.6 3.1 copy-start.5
  0.7 17.3 %copy-start.1 = (bf16[1024,1024]{1,0:T(8,128)(2,1)S(1)}, bf16[1024,1024]{1,0:T(8,128)(2,1)}, u32[]{:S(2)}) copy-start(bf16[1024,1024]{1,0:T(8,128)(2,1)} %refs_6_.17) | copy-start | bytes 6291460
  0.7 17.2 %copy-start.25 = (s32[1024]{0:T(1024)S(1)}, s32[1024]{0:T(1024)}, u32[]{:S(2)}) copy-start(s32[1024]{0:T(1024)} %param.9) | copy-start | bytes 12292
  93.9 3.0 collective-permute-start
  98.6 2.2 copy-start.13
  131.8 1.7 collective-permute-start.1
  137.5 10.5 %copy-start.12 = (f32[256,1024]{1,0:T(8,128)S(1)}, f32[256,1024]{1,0:T(8,128)}, u32[]{:S(2)}) copy-start(f32[256,1024]{1,0:T(8,128)} %copy-done.11) | copy-start | bytes 3145732
  137.5 10.5 %copy-start.14 = (f32[256,1024]{1,0:T(8,128)S(1)}, f32[256,1024]{1,0:T(8,128)}, u32[]{:S(2)}) copy-start(f32[256,1024]{1,0:T(8,128)} %copy-done.13) | copy-start | bytes 3145732
  149.1 1.8 copy-start.15
  150.9 25.1 %copy-start.24 = (f32[1024]{0:T(1024)S(1)}, f32[1024]{0:T(1024)}, u32[]{:S(2)}) copy-start(f32[1024]{0:T(1024)} %param.7) | copy-start | bytes 12292
  151.5 16.8 %collective-permute-start.2 = (f32[128,1280]{1,0:T(8,128)S(1)}, f32[128,1280]{1,0:T(8,128)S(1)}, u32[]{:S(2)}, u32[]{:S(2)}) collective-permute-start(f32[128,1280]{1,0:T(8,128)S(1)} %pad_maximum_fusion.3), channel_id=1, source_target_pairs={{0,16},{8,24},{16,0},{24,8},{1,17},{9,25},{17,1},{25,9},{2,18},{10... | collective-permute-start | bytes 1966088 | tf_op jit(solution)/shard_map/ppermute | solution.py:27
  168.3 7.6 %copy-start.20 = (f32[128,1280]{1,0:T(8,128)}, f32[128,1280]{1,0:T(8,128)S(1)}, u32[]{:S(2)}) copy-start(f32[128,1280]{1,0:T(8,128)S(1)} %collective-permute-done.2) | copy-start | bytes 1966084
  168.3 7.7 %collective-permute-start.3 = (f32[128,1280]{1,0:T(8,128)S(1)}, f32[128,1280]{1,0:T(8,128)}, u32[]{:S(2)}, u32[]{:S(2)}) collective-permute-start(f32[128,1280]{1,0:T(8,128)S(1)} %collective-permute-done.2), channel_id=1, source_target_pairs={{0,8},{8,0},{16,24},{24,16},{1,9},{9,1},{17,25},{25,17},{2,10},{10... | collective-permute-start | bytes 1966088 | tf_op jit(solution)/shard_map/ppermute | solution.py:27
  181.3 10.2 %all-to-all-start.6 = ((f32[8,8,256]{2,1,0:T(8,128)}), f32[8,8,256]{2,1,0:T(8,128)S(1)}, u32[]{:S(2)}, u32[]{:S(2)}) async-start(f32[8,8,256]{2,1,0:T(8,128)} %convolution_bitcast_fusion.1), calls=%async_computation.6 | async-start | bytes 131072 | tf_op jit(solution)/shard_map/all_to_all | solution.py:38
  192.1 9.8 %all-to-all-start.5 = ((f32[8,1,512]{2,1,0:T(1,128)}), f32[8,1,512]{2,1,0:T(1,128)S(1)}, u32[]{:S(2)}, u32[]{:S(2)}) async-start(f32[8,1,512]{2,1,0:T(1,128)} %broadcast_in_dim.21), calls=%async_computation.5 | async-start | bytes 32768 | tf_op jit(solution)/shard_map/all_to_all | solution.py:306
  202.7 13.9 %all-to-all-start.7 = ((f32[32,8,256]{2,1,0:T(8,128)}), f32[32,8,256]{2,1,0:T(8,128)}, u32[]{:S(2)}, u32[]{:S(2)}) async-start(f32[32,8,256]{2,1,0:T(8,128)} %broadcast_in_dim.22), calls=%async_computation.7 | async-start | bytes 524288 | tf_op jit(solution)/shard_map/all_to_all | solution.py:88
  206.2 1.8 copy-start.19
  219.9 10.5 %copy-start.21 = (f32[256,256]{1,0:T(8,128)S(1)}, f32[256,256]{1,0:T(8,128)}, u32[]{:S(2)}) copy-start(f32[256,256]{1,0:T(8,128)} %get-tuple-element.102) | copy-start | bytes 786436
  221.0 11.4 %copy-start.8 = (f32[256,1024]{1,0:T(8,128)S(1)}, f32[256,1024]{1,0:T(8,128)}, u32[]{:S(2)}) copy-start(f32[256,1024]{1,0:T(8,128)} %copy-done.7) | copy-start | bytes 3145732
  221.0 11.4 %copy-start.10 = (f32[256,1024]{1,0:T(8,128)S(1)}, f32[256,1024]{1,0:T(8,128)}, u32[]{:S(2)}) copy-start(f32[256,1024]{1,0:T(8,128)} %copy-done.9) | copy-start | bytes 3145732
  234.5 12.6 %copy-start.2 = (bf16[256,1024]{1,0:T(8,128)(2,1)}, bf16[256,1024]{1,0:T(8,128)(2,1)S(1)}, u32[]{:S(2)}) copy-start(bf16[256,1024]{1,0:T(8,128)(2,1)S(1)} %get-tuple-element.111.refs_4_.refs_5_.refs_7_) | copy-start | bytes 1572868
  247.1 10.1 %all-to-all-start.8 = ((f32[8,1,1408]{2,1,0:T(1,128)}), f32[8,1,1408]{2,1,0:T(1,128)S(1)}, u32[]{:S(2)}, u32[]{:S(2)}) async-start(f32[8,1,1408]{2,1,0:T(1,128)} %get-tuple-element.52), calls=%async_computation.8 | async-start | bytes 90112 | tf_op jit(solution)/shard_map/all_to_all | solution.py:331
  259.6 11.4 %all-to-all-start.9 = ((f32[32,1,1408]{2,1,0:T(1,128)}), f32[32,1,1408]{2,1,0:T(1,128)}, u32[]{:S(2)}, u32[]{:S(2)}) async-start(f32[32,1,1408]{2,1,0:T(1,128)} %bitcast.110), calls=%async_computation.9 | async-start | bytes 360448 | tf_op jit(solution)/shard_map/all_to_all | solution.py:340
  (11 other events, 11.4 us)

commit v3 on v2

--- a/solution.py
+++ b/solution.py
@@ -14,7 +14,7 @@
 shrink_share = 0.05
 highest = lax.Precision.HIGHEST
 LANES = 128
-BLOCK = 16
+BLOCK = 32
 VMEM_LIMIT = 16 * 1024 * 1024
 NT = (((1,), (1,)), ((), ()))
 NN = (((1,), (0,)), ((), ()))
@@ -29,7 +29,7 @@
 
 def shrink_weights(range_rows):
     moment = jnp.dot(range_rows.T, range_rows, precision=highest)
-    return jnp.dot(inverse_factor(moment, shrink_share), range_rows.T, precision=highest)
+    return jnp.dot(inverse_factor(moment, shrink_share), range_rows.T, precision=lax.Precision.HIGH)
 
 
 def scattered_cols(part):
@@ -54,40 +54,57 @@
     return lax.dynamic_slice_in_dim(value, index * size, size, 0)
 
 
-def leaf_gram(leaf, position):
+def leaf_gram(leaf, grad_sum, position):
     width = leaf.shape[0]
     low = position % 2 == 0
     lower, upper = in_order(low, leaf, swapped(leaf, "rows", 0))
     piece = rows_at(lower, position % 2, 2)
     share = jnp.concatenate([gram_of(leaf, leaf), gram_of(piece, upper)], 0)
+    grad_sum = grad_sum + swapped(grad_sum, "rows", 0)
+    share, grad_sum = lax.optimization_barrier((share, grad_sum))
     share = summed_blocks(share)
     first, second = in_order(low, share, swapped(share, "rows", 0))
     cross = jnp.concatenate([first[width:], second[width:]], 0)
-    return jnp.concatenate([lower, upper], 0), first[:width], second[:width], cross
+    return jnp.concatenate([lower, upper], 0), first[:width], second[:width], cross, grad_sum
 
 
 def gram_of(left, right):
-    return lax.dot_general(left, right, NT, precision=highest)
-
-
-def merge_gram(sketch, gram, position, level):
+    return lax.dot_general(left, right, NT, precision=lax.Precision.HIGH)
+
+
+def merge_gram(sketch, gram, grad_sum, gradient_of, weight, position, level):
     n_row, n_col = lax.axis_size("rows"), lax.axis_size("cols")
     width, feats = sketch.shape
     group = 1 << level
+    last = 2 * group == n_row
     both = jnp.concatenate([rows_at(sketch, position % group, group), rows_at(gram, position % group, group)], 1)
-    both = swapped(both, "rows", level)
+    grad_other = swapped(grad_sum, "rows", level)
+    both, grad_other = lax.optimization_barrier((swapped(both, "rows", level), grad_other))
+    grad_sum = grad_sum + grad_other
+    gradient = gradient_of(grad_sum)
     for bit in range(level):
         first, second = in_order(position // (1 << bit) % 2 == 0, both, swapped(both, "rows", bit))
         both = jnp.concatenate([first, second], 0)
     low = position // group % 2 == 0
     lower, upper = in_order(low, sketch, both[:, :feats])
     first, second = in_order(low, gram, both[:, feats:])
+    stacked = jnp.concatenate([lower, upper], 0)
     part = gram_of(rows_at(lower, position % (2 * group), 2 * group), upper)
     block = scattered_cols(part)
-    sent = jnp.broadcast_to(block[None], (n_row * n_col, *block.shape))
-    heard = lax.all_to_all(sent, ("rows", "cols"), 0, 0).reshape(n_row, -1, width)
-    cross = lax.dynamic_slice_in_dim(heard, position // (2 * group) * (2 * group), 2 * group, 0)
-    return jnp.concatenate([lower, upper], 0), first, second, cross.reshape(width, width)
+    pieces = [block.reshape(1, -1)]
+    if last:
+        weight_piece = rows_at(weight, lax.axis_index("cols"), n_col)
+        pieces += [gram_of(gradient[None], stacked), weight_piece[None]]
+    sent = jnp.concatenate(pieces, 1)
+    sent = jnp.broadcast_to(sent[None], (n_row * n_col, *sent.shape))
+    heard = lax.all_to_all(sent, ("rows", "cols"), 0, 0).reshape(n_row, n_col, -1)
+    start = position // (2 * group) * (2 * group)
+    cross = lax.dynamic_slice_in_dim(heard[:, :, : block.size], start, 2 * group, 0)
+    felt, weights = None, None
+    if last:
+        felt = jnp.sum(heard[0, :, block.size : block.size + 2 * width], 0)[None]
+        weights = heard[:, :, block.size + 2 * width :].reshape(n_row, 1, -1)
+    return stacked, first, second, cross.reshape(width, width), grad_sum, felt, weights
 
 
 def split(value, parts):
@@ -106,7 +123,7 @@
     m = m_ref[...]
     diag = jnp.where(row == lane, m, 0.0)
     trace = jnp.sum(jnp.sum(diag, axis=0, keepdims=True), axis=1, keepdims=True)
-    a_ref[...] = m + jnp.where(row == lane, share * trace / n, 0.0)
+    a_ref[...] = m / trace + jnp.where(row == lane, share / n, 0.0)
     sub = lax.broadcasted_iota(jnp.int32, (BLOCK, LANES), 0)
     wide_sub = lax.broadcasted_iota(jnp.int32, (BLOCK, n), 0)
     wide_lane = lax.broadcasted_iota(jnp.int32, (BLOCK, n), 1)
@@ -122,14 +139,21 @@
             inside = (wide_lane >= base) & (wide_lane < base + BLOCK)
             panel = jnp.where(inside, jnp.where(wide_lane - base == wide_sub, 1.0, 0.0), panel)
             scale = jnp.zeros((BLOCK, LANES), jnp.float32)
-            for k in range(BLOCK):
-                pivot = jnp.broadcast_to(cols[k][k : k + 1], (BLOCK, LANES))
-                inverse = 1.0 / pivot
-                scale = jnp.where(sub == k, lax.rsqrt(pivot), scale)
-                factor = jnp.where(sub > k, cols[k], 0.0) * inverse
-                panel = panel - jnp.concatenate([factor] * (n // LANES), 1) * panel[k : k + 1]
-                for m in range(k + 1, BLOCK):
-                    cols[m] = cols[m] - factor * cols[k][m : m + 1]
+            for k in range(0, BLOCK, 2):
+                top, low = cols[k], cols[k + 1]
+                a = jnp.broadcast_to(top[k : k + 1], (BLOCK, LANES))
+                b = jnp.broadcast_to(top[k + 1 : k + 2], (BLOCK, LANES))
+                c = jnp.broadcast_to(low[k + 1 : k + 2], (BLOCK, LANES))
+                det = a * c - b * b
+                inv_a, inv_det = 1.0 / a, 1.0 / det
+                scale = jnp.where(sub == k, lax.rsqrt(a), jnp.where(sub == k + 1, lax.rsqrt(det * inv_a), scale))
+                first = jnp.where(sub > k, top, 0.0) * inv_a
+                low = low - first * b
+                second = jnp.where(sub > k + 1, low, 0.0) * (a * inv_det)
+                panel = panel - jnp.concatenate([first] * (n // LANES), 1) * panel[k : k + 1]
+                panel = panel - jnp.concatenate([second] * (n // LANES), 1) * panel[k + 1 : k + 2]
+                for m in range(k + 2, BLOCK):
+                    cols[m] = cols[m] - (first * top[m : m + 1] + second * low[m : m + 1])
             panel = panel * jnp.concatenate([scale] * (n // LANES), 1)
             a_ref[pl.ds(pl.multiple_of(base, BLOCK), BLOCK), :] = panel
             after = jnp.where(wide_lane >= base + BLOCK, panel, 0.0)[:, first_row:]
@@ -138,14 +162,13 @@
             left = jnp.concatenate([l0, l0, l1, l0, l1, l2], 0)
             right = jnp.concatenate([r0, r1, r0, r2, r1, r0], 0)
             update = lax.dot_general(left, right, TN, preferred_element_type=jnp.float32)
-            old = a_ref[first_row:, :]
-            lane_here, row_here = lane[first_row:], row[first_row:]
-            gone = (lane_here >= base) & (lane_here < base + BLOCK) & (row_here >= base + BLOCK)
-            a_ref[first_row:, :] = jnp.where(gone, 0.0, old) - update
+            kept = jnp.where((wide_lane[:1] >= base) & (wide_lane[:1] < base + BLOCK), 0.0, 1.0)
+            a_ref[first_row:, :] = a_ref[first_row:, :] * kept - update
+            a_ref[pl.ds(pl.multiple_of(base, BLOCK), BLOCK), :] = panel
             return carry
 
         lax.fori_loop(0, LANES // BLOCK, step, 0)
-    w_ref[...] = jnp.where(lane <= row, a_ref[...], 0.0)
+    w_ref[...] = jnp.where(lane <= row, a_ref[...], 0.0) * lax.rsqrt(trace)
 
 def inverse_factor(m, share):
     n = m.shape[0]
@@ -232,20 +255,20 @@
     s0, s1 = s0_ref[...], s1_ref[...]
     z = (r - row_dot(stacked_splits(s), (s0, s1), NN)) / damping
     if first:
-        p = z
+        p, sp = z, samples * s
     else:
         solved = row_dot(stacked_splits(pressed), inv, NN)
         norm = total(squares) / (samples * samples) + 2.0 * damping * bending + damping * damping * length
         bent = (norm - total(pressed * solved)) / damping
-        p = z + (step * step * bent / agreement - 1.0) * p
+        beta = step * step * bent / agreement - 1.0
+        p, sp = z + beta * p, samples * s + beta * sp
     rounded = (scale_ref[...] * p).astype(jnp.bfloat16)
     ahead = lax.dot_general(
         jnp.broadcast_to(rounded, (8, rounded.shape[1])), design_ref[...], NT,
         preferred_element_type=jnp.float32,
     )[0:1]
-    sp = row_dot(stacked_splits(p), (s0, s1), NT)
     scalars = put_scalars((total(r * z), total(p * p)))
-    message = jnp.concatenate([ahead, sp, scalars], axis=1)
+    message = jnp.concatenate([ahead, scalars], axis=1)
     for col in range(msg_out.shape[0]):
         msg_out[col] = message
     vec_out[...] = jnp.zeros_like(vec_out)
@@ -254,30 +277,42 @@
     vec_out[2:3] = p
     small_out[...] = jnp.zeros_like(small_out)
     small_out[0:1] = q
-
-
-def backward_kernel(last, *refs):
-    if last:
-        (msg_ref, small_ref, weight_ref, small_out, bend_out) = refs
-    else:
-        (msg_ref, small_ref, weight_ref, scale_ref, design_ref, s0_ref, s1_ref, small_out, msg_out) = refs
+    small_out[1:2] = sp
+
+
+def last_kernel(samples, msg_ref, vec_ref, weights_ref, x_out):
+    rows = weights_ref.shape[2]
+    bend = jnp.zeros((1, rows), jnp.float32)
+    for group in range(msg_ref.shape[0]):
+        y = msg_ref[group, 0, :, :rows]
+        for col in range(1, msg_ref.shape[1]):
+            y = y + msg_ref[group, col, :, :rows]
+        inner = (weights_ref[group] * y).astype(jnp.bfloat16).astype(jnp.float32)
+        bend = bend + inner * y
+    tail = msg_ref[0, 0, :, rows:]
+    for col in range(1, msg_ref.shape[1]):
+        tail = tail + msg_ref[0, col, :, rows:]
+    at = tail.shape[1] - LANES
+    agreement, length = tail[:, at : at + 1], tail[:, at + 1 : at + 2]
+    curvature = total(bend) / samples + damping * length
+    x_out[...] = vec_ref[0:1] + agreement / curvature * vec_ref[2:3]
+
+
+def backward_kernel(*refs):
+    (msg_ref, small_ref, weight_ref, scale_ref, design_ref, s0_ref, s1_ref, small_out, msg_out) = refs
     rows = weight_ref.shape[1]
     width = small_ref.shape[1]
     sums = msg_ref[0]
     for col in range(1, msg_ref.shape[0]):
         sums = sums + msg_ref[col]
     y = sums[:, :rows]
-    rest = sums[:, rows + width :]
+    rest = sums[:, rows:]
     inner = (weight_ref[...] * y).astype(jnp.bfloat16)
     bend = total(inner.astype(jnp.float32) * y)
     at = lax.broadcasted_iota(jnp.int32, (1, width), 1)
     small_out[...] = jnp.zeros_like(small_out)
-    small_out[0:1] = small_ref[0:1]
-    small_out[1:2] = sums[:, rows : rows + width]
+    small_out[0:2] = small_ref[0:2]
     small_out[2:3] = jnp.where(at == 0, rest[:, 0:1], jnp.where(at == 1, rest[:, 1:2], 0.0))
-    if last:
-        bend_out[...] = put_scalars((bend,))
-        return
     back = lax.dot_general(
         jnp.broadcast_to(inner, (8, rows)), design_ref[...], NN, preferred_element_type=jnp.float32
     )[0:1]
@@ -310,7 +345,7 @@
     return jnp.sum(heard_cols(row), 0)
 
 
-def solve(design, weight, feature_scale, scales, gradient, sketch, q, inverse, samples):
+def solve(design, weight, weights, feature_scale, scales, gradient, sketch, q, inverse, samples):
     n_row, n_col = lax.axis_size("rows"), lax.axis_size("cols")
     rows, feats = design.shape
     width = sketch.shape[0]
@@ -320,19 +355,18 @@
     weight = weight[None]
     here = lax.axis_index("cols").astype(jnp.int32)[None]
     vec_shape, small_shape = (8, feats), (8, width)
-    ahead_shape = (n_col, 1, rows + width + LANES)
+    ahead_shape = (n_col, 1, rows + LANES)
+    last_shape = (n_row * n_col, 1, rows + LANES)
     back_shape = (n_row, n_col, 1, feats + width + LANES)
     vec, small, message = call(
         functools.partial(forward_kernel, samples, True),
         (vec_shape, small_shape, ahead_shape),
         (gradient[None], q, scale, design, s0, s1, inverse),
     )
-    for turn in range(ITERS):
+    for turn in range(1, ITERS):
         message = lax.all_to_all(message, "cols", 0, 0)
-        if turn + 1 == ITERS:
-            break
         small, message = call(
-            functools.partial(backward_kernel, False),
+            backward_kernel,
             (small_shape, back_shape),
             (message, small, weight, scale, design, s0, s1),
         )
@@ -340,18 +374,17 @@
         message = lax.all_to_all(message, ("rows", "cols"), 0, 0).reshape(back_shape)
         vec, small, message = call(
             functools.partial(forward_kernel, samples, False),
-            (vec_shape, small_shape, ahead_shape),
+            (vec_shape, small_shape, last_shape if turn + 1 == ITERS else ahead_shape),
             (here, message, vec, small, scales, scale, design, s0, s1, inverse),
             smem=1,
         )
-    small, bend = call(
-        functools.partial(backward_kernel, True),
-        (small_shape, (1, LANES)),
-        (message, small, weight),
+    message = lax.all_to_all(message, ("rows", "cols"), 0, 0)
+    (x,) = call(
+        functools.partial(last_kernel, samples),
+        ((1, feats),),
+        (message.reshape(n_row, n_col, 1, -1), vec, weights),
     )
-    bend = lax.psum(bend, "rows")[0, 0]
-    curvature = bend / samples + damping * small[2, 1]
-    return vec[0] + small[2, 0] / curvature * vec[2]
+    return x[0]
 
 
 def on_device(design, theta, feature_scale, labels, psi, phi):
@@ -367,8 +400,7 @@
     chance = jax.nn.sigmoid(margins)
     weight = chance * (1.0 - chance)
     misfit = (chance - labels.astype(jnp.float32)).astype(jnp.bfloat16)
-    summed_grad = lax.psum(jnp.dot(misfit, design, preferred_element_type=jnp.float32), "rows")
-    gradient = feature_scale * summed_grad / samples + damping * theta
+    grad_part = jnp.dot(misfit, design, preferred_element_type=jnp.float32)
     rows_scaled = (
         design.astype(jnp.float32) * jnp.sqrt(weight)[:, None] * feature_scale[None, :]
     ).astype(jnp.bfloat16)
@@ -381,23 +413,30 @@
     leaf_weights = shrink_weights(range_rows).astype(jnp.bfloat16)
     sketch = jnp.dot(leaf_weights, rows_scaled, preferred_element_type=jnp.float32)
     position = lax.axis_index("rows")
+
+    def gradient_of(grad_sum):
+        return feature_scale * grad_sum / samples + damping * theta
+
     for level in range(row_devices.bit_length() - 1):
         if level == 0:
-            stacked, first, second, cross = leaf_gram(sketch, position)
+            stacked, first, second, cross, grad_sum = leaf_gram(sketch, grad_part, position)
         else:
-            stacked, first, second, cross = merge_gram(sketch, gram, position, level)
+            stacked, first, second, cross, grad_sum, felt, weights_heard = merge_gram(
+                sketch, gram, grad_sum, gradient_of, weight, position, level
+            )
         full = jnp.concatenate(
             [jnp.concatenate([first, cross], 1), jnp.concatenate([cross.T, second], 1)], 0
         )
         weights = shrink_weights(jnp.dot(full, phi, precision=highest))
         sketch = jnp.dot(weights, stacked, precision=lax.Precision.HIGH)
-        gram = gram_of(jnp.dot(weights, full, precision=highest), weights)
-    felt = summed_cols(gram_of(gradient[None], stacked))
-    q = gram_of(felt, weights)
+        gram = lax.dot_general(
+            jnp.dot(weights, full, precision=lax.Precision.HIGH), weights, NT, precision=lax.Precision.HIGH
+        )
+    q = lax.dot_general(felt, weights, NT, precision=lax.Precision.HIGH)
     kernel = gram + damping * samples * jnp.eye(width, dtype=jnp.float32)
     factor = inverse_factor(kernel, 0.0)
     inverse = jnp.dot(factor.T, factor, precision=highest)
-    newton = solve(design, weight, feature_scale, scales, gradient, sketch, q, inverse, samples)
+    newton = solve(design, weight, weights_heard, feature_scale, scales, gradient_of(grad_sum), sketch, q, inverse, samples)
     return (newton, sketch)
 
 

time: 485 us -> 449 us (0.926)
  blocking collectives: 288 us -> 274 us
  Pallas kernels: 60.8 us -> 50.3 us
  matrix products: 36 us -> 30.5 us
    psum x2 -> x0, blocking collectives: 12.9 us -> none  [the longest x1 7.22 us: on_device(): lax.psum(jnp.dot(misfit, design, preferred_element_type=jnp.float32), 'ro...]
    all_to_all x9 -> x8, blocking collectives: 94.2 us -> 83.4 us  [solve(): message = lax.all_to_all(message, 'cols', 0, 0)]
    all_to_all x8 -> x9, blocking collectives: 78.2 us -> 88 us  [solve(): lax.all_to_all(message, ('rows', 'cols'), 0, 0).reshape(back_shape)]
    pallas_call x4, Pallas kernels: 35 us -> 28.8 us  [inverse_factor(): pl.pallas_call(functools.partial(factor_kernel, share), out_shape=jax.Sha...]
    all_to_all x3 -> x2, waiting for transfers between devices: 23.1 us -> 17 us  [the longest x1 9.83 us: merge_gram(): lax.all_to_all(sent, ('rows', 'cols'), 0, 0).reshape(n_row, n_col, -1)]
    dot_general x13, matrix products: 16.4 us -> 10.9 us  [the longest x4 6.65 us: gram_of(): return lax.dot_general(left, right, NT, precision=lax.Precision.HIGH)]
    all_to_all x3 -> x2, starting transfers between devices: 10.1 us -> 6.57 us  [the longest x1 3.51 us: merge_gram(): lax.all_to_all(sent, ('rows', 'cols'), 0, 0).reshape(n_row, n_col, -1)]
    ppermute x4 -> x6, waiting for transfers between devices: 17.3 us -> 20 us  [swapped(): return lax.ppermute(value, axis, pairs)]
  transfers between devices with their start and end apart: 9 -> 10, of which waited for: 8 -> 8; matrix products, arithmetic and copies ran while one was open for 2% -> 2% of each run, Pallas kernels for 0% -> 0%
where the time goes in v3:
time: 449 us; the launch traced here: 440 us
  blocking collectives  274 us (61%)
  Pallas kernels  50.3 us (11%)
  waiting for transfers between devices  48 us (11%)
  matrix products  30.5 us (7%)
  starting transfers between devices  15.8 us (4%)
  local copies, waits for them, and re-layouts  11.3 us (3%)
  other arithmetic  8.35 us (2%)
    all_to_all x9, blocking collectives, solve(): lax.all_to_all(message, ('rows', 'cols'), 0, 0).reshape(back_shape)  88 us
    all_to_all x8, blocking collectives, solve(): message = lax.all_to_all(message, 'cols', 0, 0)  83.4 us
    all_to_all x2, blocking collectives, scattered_cols(): return jnp.sum(lax.all_to_all(blocks, 'cols', 0, 0), 0)  44.6 us
    all_to_all x2, blocking collectives, summed_blocks(): return lax.all_to_all(sent, 'cols', 0, 0).reshape(part.shape)  43.9 us
    pallas_call x4, Pallas kernels, inverse_factor(): pl.pallas_call(functools.partial(factor_kernel, share), out_shape=jax.Sha...  28.8 us
    pallas_call x20, Pallas kernels, call(): pl.pallas_call(kernel, out_shape=[jax.ShapeDtypeStruct(shape, jnp.float32...  21.5 us
    ppermute x6, waiting for transfers between devices, swapped(): return lax.ppermute(value, axis, pairs)  20 us
    all_to_all x1, blocking collectives, heard_cols(): lax.all_to_all(jnp.broadcast_to(row[None], (n_col, *row.shape)), 'cols',...  14 us
  transfers between devices with their start and end apart: 10, of which 8 were waited for; matrix products, arithmetic and copies ran while one was open for 2% of the time, Pallas kernels for 0%

profile of v3, /device:TPU:0, one launch (start us, length us, event | category | flops | bytes accessed | tf_op | source)
XLA Modules:
  0.0 440.1 jit_solution(16805535542182532096)
XLA Ops:
  3.8 14.0 %all_to_all.130 = f32[8,1,2048]{2,1,0:T(1,128)S(1)} all-to-all(f32[8,1,2048]{2,1,0:T(1,128)S(1)} %broadcast_in_dim.19), channel_id=1, replica_groups=mesh['rows'=4,'cols'=8] {'cols'}, dimensions={0} | all-to-all | bytes 131072 | tf_op jit(solution)/shard_map/all_to_all | solution.py:341
  21.3 28.9 %all_to_all.131 = f32[8,128,256]{2,1,0:T(8,128)} all-to-all(f32[8,128,256]{2,1,0:T(8,128)} %bitcast.136), channel_id=1, replica_groups=mesh['rows'=4,'cols'=8] {'cols'}, dimensions={0} | all-to-all | bytes 2097152 | tf_op jit(solution)/shard_map/all_to_all | solution.py:38
  51.6 28.7 %all_to_all.132 = f32[8,128,256]{2,1,0:T(8,128)S(1)} all-to-all(f32[8,128,256]{2,1,0:T(8,128)S(1)} %broadcast_in_dim.20), channel_id=1, replica_groups=mesh['rows'=4,'cols'=8] {'cols'}, dimensions={0} | all-to-all | bytes 2097152 | tf_op jit(solution)/shard_map/all_to_all | solution.py:45
  100.6 15.7 %all_to_all.133 = f32[8,48,256]{2,1,0:T(8,128)S(1)} all-to-all(f32[8,48,256]{2,1,0:T(8,128)S(1)} %bitcast.131), channel_id=1, replica_groups=mesh['rows'=4,'cols'=8] {'cols'}, dimensions={0} | all-to-all | bytes 786432 | tf_op jit(solution)/shard_map/all_to_all | solution.py:38
  116.4 15.2 %all_to_all.134 = f32[8,48,256]{2,1,0:T(8,128)S(1)} all-to-all(f32[8,48,256]{2,1,0:T(8,128)S(1)} %broadcast_in_dim.21), channel_id=1, replica_groups=mesh['rows'=4,'cols'=8] {'cols'}, dimensions={0} | all-to-all | bytes 786432 | tf_op jit(solution)/shard_map/all_to_all | solution.py:45
  150.9 14.8 %collective-permute-done.4 = f32[1024]{0:T(1024)S(1)} collective-permute-done((f32[1024]{0:T(1024)S(1)}, f32[1024]{0:T(1024)S(1)}, u32[]{:S(2)}, u32[]{:S(2)}) %collective-permute-start.4) | collective-permute-done | bytes 4128 | tf_op jit(solution)/shard_map/ppermute | solution.py:27
  190.0 9.8 %all-to-all-done.6 = f32[32,1,2688]{2,1,0:T(1,128)} async-done(((f32[32,1,2688]{2,1,0:T(1,128)}), f32[32,1,2688]{2,1,0:T(1,128)}, u32[]{:S(2)}, u32[]{:S(2)}) %all-to-all-start.6) | async-done | bytes 344096 | tf_op jit(solution)/shard_map/all_to_all | solution.py:100
  237.6 9.8 %all_to_all.135 = f32[32,1,1408]{2,1,0:T(1,128)S(1)} all-to-all(f32[32,1,1408]{2,1,0:T(1,128)S(1)} %bitcast.119), channel_id=1, replica_groups=mesh['rows'=4,'cols'=8] {'rows','cols'}, dimensions={0} | all-to-all | bytes 360448 | tf_op jit(solution)/shard_map/all_to_all | solution.py:374
  248.7 10.4 %all_to_all.136.refs_0_ = f32[8,1,1152]{2,1,0:T(1,128)S(1)} all-to-all(f32[8,1,1152]{2,1,0:T(1,128)S(1)} %get-tuple-element.62), channel_id=1, replica_groups=mesh['rows'=4,'cols'=8] {'cols'}, dimensions={0} | all-to-all | bytes 73728 | tf_op jit(solution)/shard_map/all_to_all | solution.py:367
  259.8 9.8 %all_to_all.137 = f32[32,1,1408]{2,1,0:T(1,128)S(1)} all-to-all(f32[32,1,1408]{2,1,0:T(1,128)S(1)} %bitcast.120), channel_id=1, replica_groups=mesh['rows'=4,'cols'=8] {'rows','cols'}, dimensions={0} | all-to-all | bytes 360448 | tf_op jit(solution)/shard_map/all_to_all | solution.py:374
  271.0 10.6 %all_to_all.138.refs_0_ = f32[8,1,1152]{2,1,0:T(1,128)S(1)} all-to-all(f32[8,1,1152]{2,1,0:T(1,128)S(1)} %get-tuple-element.67), channel_id=1, replica_groups=mesh['rows'=4,'cols'=8] {'cols'}, dimensions={0} | all-to-all | bytes 73728 | tf_op jit(solution)/shard_map/all_to_all | solution.py:367
  282.4 9.8 %all_to_all.139 = f32[32,1,1408]{2,1,0:T(1,128)S(1)} all-to-all(f32[32,1,1408]{2,1,0:T(1,128)S(1)} %bitcast.121), channel_id=1, replica_groups=mesh['rows'=4,'cols'=8] {'rows','cols'}, dimensions={0} | all-to-all | bytes 360448 | tf_op jit(solution)/shard_map/all_to_all | solution.py:374
  293.5 10.4 %all_to_all.140.refs_0_ = f32[8,1,1152]{2,1,0:T(1,128)S(1)} all-to-all(f32[8,1,1152]{2,1,0:T(1,128)S(1)} %get-tuple-element.72), channel_id=1, replica_groups=mesh['rows'=4,'cols'=8] {'cols'}, dimensions={0} | all-to-all | bytes 73728 | tf_op jit(solution)/shard_map/all_to_all | solution.py:367
  304.7 9.8 %all_to_all.141 = f32[32,1,1408]{2,1,0:T(1,128)S(1)} all-to-all(f32[32,1,1408]{2,1,0:T(1,128)S(1)} %bitcast.122), channel_id=1, replica_groups=mesh['rows'=4,'cols'=8] {'rows','cols'}, dimensions={0} | all-to-all | bytes 360448 | tf_op jit(solution)/shard_map/all_to_all | solution.py:374
  315.8 10.4 %all_to_all.142.refs_0_ = f32[8,1,1152]{2,1,0:T(1,128)S(1)} all-to-all(f32[8,1,1152]{2,1,0:T(1,128)S(1)} %get-tuple-element.77), channel_id=1, replica_groups=mesh['rows'=4,'cols'=8] {'cols'}, dimensions={0} | all-to-all | bytes 73728 | tf_op jit(solution)/shard_map/all_to_all | solution.py:367
  326.9 9.8 %all_to_all.143 = f32[32,1,1408]{2,1,0:T(1,128)S(1)} all-to-all(f32[32,1,1408]{2,1,0:T(1,128)S(1)} %bitcast.123), channel_id=1, replica_groups=mesh['rows'=4,'cols'=8] {'rows','cols'}, dimensions={0} | all-to-all | bytes 360448 | tf_op jit(solution)/shard_map/all_to_all | solution.py:374
  338.1 10.4 %all_to_all.144.refs_0_ = f32[8,1,1152]{2,1,0:T(1,128)S(1)} all-to-all(f32[8,1,1152]{2,1,0:T(1,128)S(1)} %get-tuple-element.82), channel_id=1, replica_groups=mesh['rows'=4,'cols'=8] {'cols'}, dimensions={0} | all-to-all | bytes 73728 | tf_op jit(solution)/shard_map/all_to_all | solution.py:367
  349.2 9.8 %all_to_all.145 = f32[32,1,1408]{2,1,0:T(1,128)S(1)} all-to-all(f32[32,1,1408]{2,1,0:T(1,128)S(1)} %bitcast.124), channel_id=1, replica_groups=mesh['rows'=4,'cols'=8] {'rows','cols'}, dimensions={0} | all-to-all | bytes 360448 | tf_op jit(solution)/shard_map/all_to_all | solution.py:374
  360.3 10.4 %all_to_all.146.refs_0_ = f32[8,1,1152]{2,1,0:T(1,128)S(1)} all-to-all(f32[8,1,1152]{2,1,0:T(1,128)S(1)} %get-tuple-element.87), channel_id=1, replica_groups=mesh['rows'=4,'cols'=8] {'cols'}, dimensions={0} | all-to-all | bytes 73728 | tf_op jit(solution)/shard_map/all_to_all | solution.py:367
  371.5 9.8 %all_to_all.147 = f32[32,1,1408]{2,1,0:T(1,128)S(1)} all-to-all(f32[32,1,1408]{2,1,0:T(1,128)S(1)} %bitcast.125), channel_id=1, replica_groups=mesh['rows'=4,'cols'=8] {'rows','cols'}, dimensions={0} | all-to-all | bytes 360448 | tf_op jit(solution)/shard_map/all_to_all | solution.py:374
  382.6 10.4 %all_to_all.148.refs_0_ = f32[8,1,1152]{2,1,0:T(1,128)S(1)} all-to-all(f32[8,1,1152]{2,1,0:T(1,128)S(1)} %get-tuple-element.92), channel_id=1, replica_groups=mesh['rows'=4,'cols'=8] {'cols'}, dimensions={0} | all-to-all | bytes 73728 | tf_op jit(solution)/shard_map/all_to_all | solution.py:367
  393.8 9.8 %all_to_all.149 = f32[32,1,1408]{2,1,0:T(1,128)S(1)} all-to-all(f32[32,1,1408]{2,1,0:T(1,128)S(1)} %bitcast.126), channel_id=1, replica_groups=mesh['rows'=4,'cols'=8] {'rows','cols'}, dimensions={0} | all-to-all | bytes 360448 | tf_op jit(solution)/shard_map/all_to_all | solution.py:374
  404.9 10.4 %all_to_all.150.refs_0_ = f32[8,1,1152]{2,1,0:T(1,128)S(1)} all-to-all(f32[8,1,1152]{2,1,0:T(1,128)S(1)} %get-tuple-element.97), channel_id=1, replica_groups=mesh['rows'=4,'cols'=8] {'cols'}, dimensions={0} | all-to-all | bytes 73728 | tf_op jit(solution)/shard_map/all_to_all | solution.py:367
  416.1 9.8 %all_to_all.151 = f32[32,1,1408]{2,1,0:T(1,128)S(1)} all-to-all(f32[32,1,1408]{2,1,0:T(1,128)S(1)} %bitcast.118), channel_id=1, replica_groups=mesh['rows'=4,'cols'=8] {'rows','cols'}, dimensions={0} | all-to-all | bytes 360448 | tf_op jit(solution)/shard_map/all_to_all | solution.py:374
  (161 shorter events, 139.6 us)
Async XLA Ops:
  0.6 17.3 %copy-start = (bf16[1024,256]{1,0:T(8,128)(2,1)S(1)}, bf16[1024,256]{1,0:T(8,128)(2,1)}, u32[]{:S(2)}) copy-start(bf16[1024,256]{1,0:T(8,128)(2,1)} %param.10) | copy-start | bytes 1572868
  0.6 3.1 copy-start.4
  0.7 17.3 %copy-start.1 = (bf16[1024,1024]{1,0:T(8,128)(2,1)S(1)}, bf16[1024,1024]{1,0:T(8,128)(2,1)}, u32[]{:S(2)}) copy-start(bf16[1024,1024]{1,0:T(8,128)(2,1)} %refs_6_.17) | copy-start | bytes 6291460
  0.7 17.2 %copy-start.26 = (s32[1024]{0:T(1024)S(1)}, s32[1024]{0:T(1024)}, u32[]{:S(2)}) copy-start(s32[1024]{0:T(1024)} %param.9) | copy-start | bytes 12292
  91.9 5.3 %collective-permute-start = (f32[256,1024]{1,0:T(8,128)}, f32[256,1024]{1,0:T(8,128)}, u32[]{:S(2)}, u32[]{:S(2)}) collective-permute-start(f32[256,1024]{1,0:T(8,128)} %fusion.11), channel_id=1, source_target_pairs={{0,8},{8,0},{16,24},{24,16},{1,9},{9,1},{17,25},{25,17},{2,10},{10... | collective-permute-start | bytes 3145736 | tf_op jit(solution)/shard_map/ppermute | solution.py:27
  92.3 2.6 collective-permute-start.1
  131.6 1.7 collective-permute-start.2
  137.2 8.7 %copy-start.11 = (f32[256,1024]{1,0:T(8,128)S(1)}, f32[256,1024]{1,0:T(8,128)}, u32[]{:S(2)}) copy-start(f32[256,1024]{1,0:T(8,128)} %copy-done.10) | copy-start | bytes 3145732
  137.2 8.7 %copy-start.13 = (f32[256,1024]{1,0:T(8,128)S(1)}, f32[256,1024]{1,0:T(8,128)}, u32[]{:S(2)}) copy-start(f32[256,1024]{1,0:T(8,128)} %copy-done.12) | copy-start | bytes 3145732
  147.7 18.1 %copy-start.25 = (f32[1024]{0:T(1024)S(1)}, f32[1024]{0:T(1024)}, u32[]{:S(2)}) copy-start(f32[1024]{0:T(1024)} %param.7) | copy-start | bytes 12292
  148.9 16.9 %collective-permute-start.3 = (f32[128,1280]{1,0:T(8,128)S(1)}, f32[128,1280]{1,0:T(8,128)S(1)}, u32[]{:S(2)}, u32[]{:S(2)}) collective-permute-start(f32[128,1280]{1,0:T(8,128)S(1)} %pad_maximum_fusion.3), channel_id=1, source_target_pairs={{0,16},{8,24},{16,0},{24,8},{1,17},{9,25},{17,1},{25,9},{2,18},{10... | collective-permute-start | bytes 1966088 | tf_op jit(solution)/shard_map/ppermute | solution.py:27
  150.3 15.4 %collective-permute-start.4 = (f32[1024]{0:T(1024)S(1)}, f32[1024]{0:T(1024)S(1)}, u32[]{:S(2)}, u32[]{:S(2)}) collective-permute-start(f32[1024]{0:T(1024)S(1)} %add.60), channel_id=1, source_target_pairs={{0,16},{8,24},{16,0},{24,8},{1,17},{9,25},{17,1},{25,9},{2,18},{10... | collective-permute-start | bytes 12296 | tf_op jit(solution)/shard_map/ppermute | solution.py:27
  165.7 2.2 collective-permute-start.5
  165.8 3.6 copy-start.15
  172.8 10.2 %all-to-all-start.5 = ((f32[8,8,256]{2,1,0:T(8,128)}), f32[8,8,256]{2,1,0:T(8,128)S(1)}, u32[]{:S(2)}, u32[]{:S(2)}) async-start(f32[8,8,256]{2,1,0:T(8,128)} %convolution_bitcast_fusion.1), calls=%async_computation.5 | async-start | bytes 131072 | tf_op jit(solution)/shard_map/all_to_all | solution.py:38
  184.0 15.9 %all-to-all-start.6 = ((f32[32,1,2688]{2,1,0:T(1,128)}), f32[32,1,2688]{2,1,0:T(1,128)}, u32[]{:S(2)}, u32[]{:S(2)}) async-start(f32[32,1,2688]{2,1,0:T(1,128)} %broadcast_in_dim.49), calls=%async_computation.6 | async-start | bytes 688128 | tf_op jit(solution)/shard_map/all_to_all | solution.py:100
  187.5 1.8 copy-start.18
  189.3 12.5 %copy-start.21 = (f32[256,256]{1,0:T(8,128)S(1)}, f32[256,256]{1,0:T(8,128)}, u32[]{:S(2)}) copy-start(f32[256,256]{1,0:T(8,128)} %get-tuple-element.104) | copy-start | bytes 786436
  203.9 8.7 %copy-start.24 = (f32[256,256]{1,0:T(8,128)S(1)}, f32[256,256]{1,0:T(8,128)}, u32[]{:S(2)}) copy-start(f32[256,256]{1,0:T(8,128)} %broadcast_select_fusion.8) | copy-start | bytes 786436
  205.0 8.3 %copy-start.7 = (f32[256,1024]{1,0:T(8,128)S(1)}, f32[256,1024]{1,0:T(8,128)}, u32[]{:S(2)}) copy-start(f32[256,1024]{1,0:T(8,128)} %copy-done.6) | copy-start | bytes 3145732
  205.0 8.3 %copy-start.9 = (f32[256,1024]{1,0:T(8,128)S(1)}, f32[256,1024]{1,0:T(8,128)}, u32[]{:S(2)}) copy-start(f32[256,1024]{1,0:T(8,128)} %copy-done.8) | copy-start | bytes 3145732
  215.4 10.3 %copy-start.2 = (bf16[256,1024]{1,0:T(8,128)(2,1)}, bf16[256,1024]{1,0:T(8,128)(2,1)S(1)}, u32[]{:S(2)}) copy-start(bf16[256,1024]{1,0:T(8,128)(2,1)S(1)} %get-tuple-element.113.refs_4_.refs_5_.refs_7_) | copy-start | bytes 1572868
  225.8 10.0 %all-to-all-start.7 = ((f32[8,1,1152]{2,1,0:T(1,128)}), f32[8,1,1152]{2,1,0:T(1,128)S(1)}, u32[]{:S(2)}, u32[]{:S(2)}) async-start(f32[8,1,1152]{2,1,0:T(1,128)} %get-tuple-element.57), calls=%async_computation.7 | async-start | bytes 73728 | tf_op jit(solution)/shard_map/all_to_all | solution.py:367
  427.9 11.0 %all-to-all-start.25 = ((f32[32,1,1152]{2,1,0:T(1,128)}), f32[32,1,1152]{2,1,0:T(1,128)S(1)}, u32[]{:S(2)}, u32[]{:S(2)}) async-start(f32[32,1,1152]{2,1,0:T(1,128)} %copy-done.5), calls=%async_computation.25 | async-start | bytes 294912 | tf_op jit(solution)/shard_map/all_to_all | solution.py:381
  (13 other events, 13.1 us)
